TPU v7x, 32 devices: a whole 2x2x4 slice. The times are simulated.
32 devices in a mesh: ty: 8 (over z, y), tx: 4 (over x, core).
Axes of the slice: x: 2, y: 2, z: 4, core: 2. Of those that a mesh axis runs over, the one named last changes fastest.
Arguments:
- x_tok: bfloat16 [2048, 2560], P('ty', 'tx')
- dy_tok: bfloat16 [2048, 2560], P('ty', 'tx')
- ln_gain: float32 [2560], P('tx')
- w_gate: bfloat16 [2560, 10240], P('tx', 'ty')
- w_up: bfloat16 [2560, 10240], P('tx', 'ty')
- w_down: bfloat16 [10240, 2560], P('ty', 'tx')
Outputs:
- output 1: bfloat16 [2048, 2560], P('ty', 'tx')
- output 2: bfloat16 [2048, 2560], P('ty', 'tx')
- output 3: float32 [2560, 10240], P('tx', 'ty')
- output 4: float32 [2560, 10240], P('tx', 'ty')
- output 5: float32 [10240, 2560], P('ty', 'tx')
- output 6: float32 [2560], P('tx')
All inputs are finite; a program needn't handle non-finite values.
Results may differ from a plain program's by a relative error of at most 0.00128048.
Values are sent between devices in bfloat16 or wider.
A program may use at most 1 GiB of HBM per device.

v0:
```python
import jax
import jax.numpy as jnp
from jax import lax
from jax.sharding import PartitionSpec as P

LN_EPS = 1e-6


def contract_rows(left_op, right_op):
    return lax.dot_general(left_op, right_op, (((0,), (0,)), ((), ())), preferred_element_type=jnp.float32)


def contract_cols(left_op, right_op):
    return lax.dot_general(left_op, right_op, (((1,), (1,)), ((), ())), preferred_element_type=jnp.float32)


def solution(mesh):
    tx_size = mesh.shape["tx"]

    def local_step(x_blk, dy_blk, gain_blk, w_gate_blk, w_up_blk, w_down_blk):
        d_model = x_blk.shape[1] * tx_size
        x_float = x_blk.astype(jnp.float32)
        ln_stats = lax.psum(jnp.stack([jnp.sum(x_float, axis=1), jnp.sum(x_float * x_float, axis=1)]), "tx") / d_model
        mean_x = ln_stats[0][:, None]
        inv_std = lax.rsqrt(ln_stats[1][:, None] - mean_x * mean_x + LN_EPS)
        x_hat = (x_float - mean_x) * inv_std
        h_blk = (gain_blk * x_hat).astype(jnp.bfloat16)
        h_all = lax.all_gather(h_blk, "ty", axis=0, tiled=True)
        gate_pre = lax.psum_scatter(jnp.dot(h_all, w_gate_blk, preferred_element_type=jnp.float32),
                                    "tx", scatter_dimension=0, tiled=True)
        up_pre = lax.psum_scatter(jnp.dot(h_all, w_up_blk, preferred_element_type=jnp.float32),
                                  "tx", scatter_dimension=0, tiled=True)
        gate_sig = jax.nn.sigmoid(gate_pre)
        gate_swish = gate_pre * gate_sig
        act_blk = (gate_swish * up_pre).astype(jnp.bfloat16)
        act_all = lax.all_gather(act_blk, "tx", axis=0, tiled=True)
        mlp_out = lax.psum_scatter(jnp.dot(act_all, w_down_blk, preferred_element_type=jnp.float32),
                                   "ty", scatter_dimension=0, tiled=True)
        y_blk = (x_float + mlp_out).astype(jnp.bfloat16)

        dy_all = lax.all_gather(dy_blk, "ty", axis=0, tiled=True)
        dw_down_blk = contract_rows(act_all, dy_all)
        d_act = lax.psum_scatter(contract_cols(dy_all, w_down_blk), "tx", scatter_dimension=0, tiled=True)
        d_gate = (d_act * up_pre * gate_sig * (1.0 + gate_pre * (1.0 - gate_sig))).astype(jnp.bfloat16)
        d_up = (d_act * gate_swish).astype(jnp.bfloat16)
        d_gate_all = lax.all_gather(d_gate, "tx", axis=0, tiled=True)
        d_up_all = lax.all_gather(d_up, "tx", axis=0, tiled=True)
        dw_gate_blk = contract_rows(h_all, d_gate_all)
        dw_up_blk = contract_rows(h_all, d_up_all)
        d_hnorm = lax.psum_scatter(contract_cols(d_gate_all, w_gate_blk) + contract_cols(d_up_all, w_up_blk),
                                   "ty", scatter_dimension=0, tiled=True)
        value_a6 = d_hnorm * gain_blk
        bwd_stats = lax.psum(jnp.stack([jnp.sum(value_a6, axis=1), jnp.sum(value_a6 * x_hat, axis=1)]), "tx") / d_model
        dx_ln = inv_std * (value_a6 - bwd_stats[0][:, None] - x_hat * bwd_stats[1][:, None])
        dx_blk = (dy_blk.astype(jnp.float32) + dx_ln).astype(jnp.bfloat16)
        d_gain_blk = lax.psum(jnp.sum(d_hnorm * x_hat, axis=0), "ty")
        return (y_blk, dx_blk, dw_gate_blk, dw_up_blk, dw_down_blk, d_gain_blk)

    return jax.shard_map(
        local_step, mesh=mesh,
        in_specs=(P("ty", "tx"), P("ty", "tx"), P("tx"), P("tx", "ty"), P("tx", "ty"), P("ty", "tx")),
        out_specs=(P("ty", "tx"), P("ty", "tx"), P("tx", "ty"), P("tx", "ty"), P("ty", "tx"), P("tx")),
        check_vma=False)
```

profile of v0, /device:TPU:0, one launch (start us, length us, event | category | flops | bytes accessed | tf_op | source)
XLA Modules:
  0.0 740.3 jit_solution(1362434666880182198)
XLA Ops:
  7.2 0.0 copy-start
  7.2 0.0 all-gather.6.cloned.1.call-start
  7.2 1.3 convert_reduce_fusion
  8.5 8.4 %psum.21 = f32[2,256]{1,0:T(2,128)S(1)} all-reduce(f32[2,256]{1,0:T(2,128)S(1)} %pad_maximum_fusion), channel_id=1, replica_groups=mesh['ty'=8,'tx'=4] {'tx'}, use_global_device_ids=true, to_apply=%region_2.0 | all-reduce | flops 512 | bytes 4096 | tf_op jit(solution)/shard_map/psum | solution.py:23
  17.0 1.9 fusion.7
  18.9 0.0 all-gather.6.cloned.1.call-update
  18.9 0.0 all-gather.10.cloned.1.call-start
  19.0 0.7 all-gather.10.cloned.1.call-update
  19.7 0.0 reduce-scatter.8.cloned.1.call-start
  19.7 54.0 %all-gather.6.cloned.1.call-done = bf16[2048,640]{1,0:T(8,128)(2,1)} async-done(((bf16[256,640]{1,0:T(8,128)(2,1)}), bf16[2048,640]{1,0:T(8,128)(2,1)}) %all-gather.6.cloned.1.call-update) | async-done | bytes 2621456 | tf_op jit(solution)/shard_map/all_gather | solution.py:28
  73.7 10.5 %fusion.18 = f32[2048,1280]{1,0:T(8,128)} fusion(bf16[2048,640]{1,0:T(8,128)(2,1)} %all-gather.6.cloned.1.call-done, bf16[640,1280]{1,0:T(8,128)(2,1)} %param.10), kind=kOutput, calls=%fused_computation.33 | convolution fusion | flops 3355443200 | bytes 14745600 | tf_op jit(solution)/shard_map/dot_general | solution.py:31
  84.1 0.0 reduce-scatter.8.cloned.1.call-update
  84.2 0.0 reduce-scatter.6.cloned.1.call-start
  84.2 9.2 %fusion.17 = f32[2048,1280]{1,0:T(8,128)} fusion(bf16[2048,640]{1,0:T(8,128)(2,1)} %all-gather.6.cloned.1.call-done, bf16[640,1280]{1,0:T(8,128)(2,1)S(1)} %copy-done), kind=kOutput, calls=%fused_computation.32 | convolution fusion | flops 3355443200 | bytes 14745600 | tf_op jit(solution)/shard_map/dot_general | solution.py:29
  93.4 0.0 reduce-scatter.6.cloned.1.call-update
  93.4 0.0 reduce-scatter.12.cloned.1.call-start
  93.5 35.6 %all-gather.10.cloned.1.call-done = bf16[2048,640]{1,0:T(8,128)(2,1)} async-done(((bf16[256,640]{1,0:T(8,128)(2,1)}), bf16[2048,640]{1,0:T(8,128)(2,1)}) %all-gather.10.cloned.1.call-update) | async-done | bytes 2621456 | tf_op jit(solution)/shard_map/all_gather | solution.py:41
  129.1 10.4 %fusion.20 = f32[2048,1280]{1,0:T(8,128)} fusion(bf16[2048,640]{1,0:T(8,128)(2,1)} %all-gather.10.cloned.1.call-done, bf16[1280,640]{1,0:T(8,128)(2,1)} %param.11), kind=kOutput, calls=%fused_computation.35 | convolution fusion | flops 3355443200 | bytes 14745600 | tf_op jit(solution)/shard_map/dot_general | solution.py:14
  139.5 0.0 reduce-scatter.12.cloned.1.call-update
  139.5 0.3 all-gather.12.cloned.1.call-start
  139.9 74.2 %reduce-scatter.8.cloned.1.call-done = f32[512,1280]{1,0:T(8,128)} async-done(((f32[2048,1280]{1,0:T(8,128)}), f32[512,1280]{1,0:T(8,128)}) %reduce-scatter.8.cloned.1.call-update) | async-done | bytes 2621456 | tf_op jit(solution)/shard_map/reduce_scatter | solution.py:31
  214.0 85.9 %reduce-scatter.6.cloned.1.call-done = f32[512,1280]{1,0:T(8,128)} async-done(((f32[2048,1280]{1,0:T(8,128)}), f32[512,1280]{1,0:T(8,128)}) %reduce-scatter.6.cloned.1.call-update) | async-done | bytes 2621456 | tf_op jit(solution)/shard_map/reduce_scatter | solution.py:29
  299.9 85.9 %reduce-scatter.12.cloned.1.call-done = f32[512,1280]{1,0:T(8,128)} async-done(((f32[2048,1280]{1,0:T(8,128)}), f32[512,1280]{1,0:T(8,128)}) %reduce-scatter.12.cloned.1.call-update) | async-done | bytes 2621456 | tf_op jit(solution)/shard_map/reduce_scatter | solution.py:43
  385.8 6.8 multiply_convert_fusion
  392.6 0.0 all-gather.12.cloned.1.call-update
  392.6 0.0 all-gather.14.cloned.1.call-start
  392.7 0.7 all-gather.14.cloned.1.call-update
  393.4 0.0 all-gather.8.cloned.1.call-start
  393.4 0.7 all-gather.8.cloned.1.call-update
  394.1 0.0 reduce-scatter.14.cloned.1.call-start
  394.2 38.9 %all-gather.12.cloned.1.call-done = bf16[2048,1280]{1,0:T(8,128)(2,1)} async-done(((bf16[512,1280]{1,0:T(8,128)(2,1)}), bf16[2048,1280]{1,0:T(8,128)(2,1)}) %all-gather.12.cloned.1.call-update) | async-done | bytes 5242896 | tf_op jit(solution)/shard_map/all_gather | solution.py:46
  433.1 9.1 %fusion.21 = f32[2048,640]{1,0:T(8,128)} fusion(bf16[2048,1280]{1,0:T(8,128)(2,1)} %all-gather.12.cloned.1.call-done, bf16[640,1280]{1,0:T(8,128)(2,1)S(1)} %copy-done), kind=kOutput, calls=%fused_computation.36 | convolution fusion | flops 3355443200 | bytes 12124160 | tf_op jit(solution)/shard_map/dot_general | solution.py:14
  442.2 33.4 %all-gather.14.cloned.1.call-done = bf16[2048,1280]{1,0:T(8,128)(2,1)} async-done(((bf16[512,1280]{1,0:T(8,128)(2,1)}), bf16[2048,1280]{1,0:T(8,128)(2,1)}) %all-gather.14.cloned.1.call-update) | async-done | bytes 5242896 | tf_op jit(solution)/shard_map/all_gather | solution.py:47
  475.6 11.1 %convolution_add_fusion = f32[2048,640]{1,0:T(8,128)} fusion(f32[2048,640]{1,0:T(8,128)} %fusion.21, bf16[2048,1280]{1,0:T(8,128)(2,1)} %all-gather.14.cloned.1.call-done, bf16[640,1280]{1,0:T(8,128)(2,1)} %param.10), kind=kOutput, calls=%fused_computation | convolution fusion | flops 3356753920 | bytes 17367040 | tf_op jit(solution)/shard_map/dot_general | solution.py:14
  486.8 0.0 reduce-scatter.14.cloned.1.call-update
  486.8 0.5 reduce-scatter.10.cloned.1.call-start
  487.3 30.8 %all-gather.8.cloned.1.call-done = bf16[2048,1280]{1,0:T(8,128)(2,1)} async-done(((bf16[512,1280]{1,0:T(8,128)(2,1)}), bf16[2048,1280]{1,0:T(8,128)(2,1)}) %all-gather.8.cloned.1.call-update) | async-done | bytes 5242896 | tf_op jit(solution)/shard_map/all_gather | solution.py:36
  518.1 9.0 %fusion.19 = f32[2048,640]{1,0:T(8,128)} fusion(bf16[2048,1280]{1,0:T(8,128)(2,1)} %all-gather.8.cloned.1.call-done, bf16[1280,640]{1,0:T(8,128)(2,1)S(1)} %copy-done.6), kind=kOutput, calls=%fused_computation.34 | convolution fusion | flops 3355443200 | bytes 12124160 | tf_op jit(solution)/shard_map/dot_general | solution.py:37
  527.1 0.0 reduce-scatter.10.cloned.1.call-update
  527.2 9.5 %fusion.24 = f32[1280,640]{1,0:T(8,128)} fusion(bf16[2048,1280]{1,0:T(8,128)(2,1)} %all-gather.8.cloned.1.call-done, bf16[2048,640]{1,0:T(8,128)(2,1)} %all-gather.10.cloned.1.call-done), kind=kOutput, calls=%fused_computation.39 | convolution fusion | flops 3355443200 | bytes 11141120 | tf_op jit(solution)/shard_map/dot_general | solution.py:10
  536.6 8.0 %fusion.22 = f32[640,1280]{1,0:T(8,128)} fusion(bf16[2048,640]{1,0:T(8,128)(2,1)S(1)} %copy-done.5, bf16[2048,1280]{1,0:T(8,128)(2,1)} %all-gather.12.cloned.1.call-done), kind=kOutput, calls=%fused_computation.37 | convolution fusion | flops 3355443200 | bytes 11141120 | tf_op jit(solution)/shard_map/dot_general | solution.py:10
  544.6 5.6 fusion.23
  550.3 74.4 %reduce-scatter.14.cloned.1.call-done = f32[256,640]{1,0:T(8,128)} async-done(((f32[2048,640]{1,0:T(8,128)}), f32[256,640]{1,0:T(8,128)}) %reduce-scatter.14.cloned.1.call-update) | async-done | bytes 655376 | tf_op jit(solution)/shard_map/reduce_scatter | solution.py:50
  624.7 1.4 fusion.13
  626.2 20.8 %psum.23 = f32[640]{0:T(1024)} all-reduce(f32[640]{0:T(1024)S(1)} %get-tuple-element.6), channel_id=1, replica_groups=mesh['ty'=8,'tx'=4] {'ty'}, use_global_device_ids=true, to_apply=%region_12.0 | all-reduce | flops 640 | bytes 5120 | tf_op jit(solution)/shard_map/psum | solution.py:56
  647.0 6.0 psum.22
  653.0 77.9 %reduce-scatter.10.cloned.1.call-done = f32[256,640]{1,0:T(8,128)} async-done(((f32[2048,640]{1,0:T(8,128)}), f32[256,640]{1,0:T(8,128)}) %reduce-scatter.10.cloned.1.call-update) | async-done | bytes 655376 | tf_op jit(solution)/shard_map/reduce_scatter | solution.py:37
  730.9 2.4 fusion.12
  (25 shorter events, 0.1 us)
Async XLA Ops:
  7.2 77.1 %copy-start = (bf16[640,1280]{1,0:T(8,128)(2,1)S(1)}, bf16[640,1280]{1,0:T(8,128)(2,1)}, u32[]{:S(2)}) copy-start(bf16[640,1280]{1,0:T(8,128)(2,1)} %param.9) | copy-start | bytes 4915204
  7.2 66.5 %all-gather.6.cloned.1.call-start = ((), (), s32[]{:S(2)}) async-start(), calls=%async_computation.5 | async-start | bytes 2949120 | tf_op jit(solution)/shard_map/all_gather | solution.py:28
  18.9 110.2 %all-gather.10.cloned.1.call-start = ((), (), s32[]{:S(2)}) async-start(), calls=%async_computation.10 | async-start | bytes 2949120 | tf_op jit(solution)/shard_map/all_gather | solution.py:41
  19.7 194.4 %reduce-scatter.8.cloned.1.call-start = ((), (), s32[]{:S(2)}) async-start(), calls=%async_computation.7 | async-start | bytes 13107200 | tf_op jit(solution)/shard_map/reduce_scatter | solution.py:31
  84.2 215.8 %reduce-scatter.6.cloned.1.call-start = ((), (), s32[]{:S(2)}) async-start(), calls=%async_computation.6 | async-start | bytes 13107200 | tf_op jit(solution)/shard_map/reduce_scatter | solution.py:29
  93.4 292.4 %reduce-scatter.12.cloned.1.call-start = ((), (), s32[]{:S(2)}) async-start(), calls=%async_computation.11 | async-start | bytes 13107200 | tf_op jit(solution)/shard_map/reduce_scatter | solution.py:43
  139.5 293.6 %all-gather.12.cloned.1.call-start = ((), (), s32[]{:S(2)}) async-start(), calls=%async_computation.12 | async-start | bytes 6553600 | tf_op jit(solution)/shard_map/all_gather | solution.py:46
  392.6 83.0 %all-gather.14.cloned.1.call-start = ((), (), s32[]{:S(2)}) async-start(), calls=%async_computation.13 | async-start | bytes 6553600 | tf_op jit(solution)/shard_map/all_gather | solution.py:47
  393.4 124.7 %all-gather.8.cloned.1.call-start = ((), (), s32[]{:S(2)}) async-start(), calls=%async_computation.8 | async-start | bytes 6553600 | tf_op jit(solution)/shard_map/all_gather | solution.py:36
  394.1 230.6 %reduce-scatter.14.cloned.1.call-start = ((), (), s32[]{:S(2)}) async-start(), calls=%async_computation.14 | async-start | bytes 5898240 | tf_op jit(solution)/shard_map/reduce_scatter | solution.py:50
  486.7 31.4 %copy-start.6 = (bf16[1280,640]{1,0:T(8,128)(2,1)S(1)}, bf16[1280,640]{1,0:T(8,128)(2,1)}, u32[]{:S(2)}) copy-start(bf16[1280,640]{1,0:T(8,128)(2,1)} %param.11) | copy-start | bytes 4915204
  486.8 244.2 %reduce-scatter.10.cloned.1.call-start = ((), (), s32[]{:S(2)}) async-start(), calls=%async_computation.9 | async-start | bytes 5898240 | tf_op jit(solution)/shard_map/reduce_scatter | solution.py:37
  527.2 9.5 %copy-start.5 = (bf16[2048,640]{1,0:T(8,128)(2,1)S(1)}, bf16[2048,640]{1,0:T(8,128)(2,1)}, u32[]{:S(2)}) copy-start(bf16[2048,640]{1,0:T(8,128)(2,1)} %all-gather.6.cloned.1.call-done) | copy-start | bytes 7864324
  527.2 17.4 %slice-start = ((s8[5242880]{0:T(1024)(128)(4,1)}), s8[4194304]{0:T(1024)(128)(4,1)S(1)}, s32[]{:S(2)}) async-start(s8[5242880]{0:T(1024)(128)(4,1)} %bitcast.37), calls=%async_computation.15 | async-start | bytes 8388608
  536.6 8.0 %slice-start.1 = ((s8[5242880]{0:T(1024)(128)(4,1)}), s8[1048576]{0:T(1024)(128)(4,1)S(1)}, s32[]{:S(2)}) async-start(s8[5242880]{0:T(1024)(128)(4,1)} %bitcast.37), calls=%async_computation.16 | async-start | bytes 2097152
  544.6 80.1 %copy-start.2 = (bf16[256,640]{1,0:T(8,128)(2,1)S(1)}, bf16[256,640]{1,0:T(8,128)(2,1)}, u32[]{:S(2)}) copy-start(bf16[256,640]{1,0:T(8,128)(2,1)} %param.6) | copy-start | bytes 983044
  544.6 80.1 %copy-start.4 = (f32[640]{0:T(1024)S(1)}, f32[640]{0:T(1024)}, u32[]{:S(2)}) copy-start(f32[640]{0:T(1024)} %param.8) | copy-start | bytes 7684
  544.6 186.3 %copy-start.3 = (bf16[256,640]{1,0:T(8,128)(2,1)S(1)}, bf16[256,640]{1,0:T(8,128)(2,1)}, u32[]{:S(2)}) copy-start(bf16[256,640]{1,0:T(8,128)(2,1)} %param.7) | copy-start | bytes 983044
  544.6 188.7 %copy-start.1 = (bf16[640,1280]{1,0:T(8,128)(2,1)S(1)}, bf16[640,1280]{1,0:T(8,128)(2,1)}, u32[]{:S(2)}) copy-start(bf16[640,1280]{1,0:T(8,128)(2,1)} %param.9) | copy-start | bytes 4915204
Sparse Core Ops, SparseCore 0:
  19.0 54.6 all-gather.5
  75.9 53.1 all-gather.9
  131.7 82.2 reduce-scatter.7
  216.5 83.4 reduce-scatter.5
  302.4 83.4 reduce-scatter.11
  392.8 40.3 all-gather.11
  435.3 40.3 all-gather.13
  477.8 40.3 all-gather.7
  521.7 102.9 reduce-scatter.13
  628.1 102.7 reduce-scatter.9
where the time goes:
time: 748 us; the launch traced here: 740 us
  waiting for transfers between devices  593 us (79%)
  matrix products  82.3 us (11%)
  blocking collectives  35.3 us (5%)
  between operations  14.4 us (2%)
  other arithmetic  13.9 us (2%)
    reduce_scatter x1, waiting for transfers between devices, local_step(): lax.psum_scatter(jnp.dot(h_all, w_gate_blk, preferred_element_type=jnp.fl...  85.9 us
    reduce_scatter x1, waiting for transfers between devices, local_step(): lax.psum_scatter(contract_cols(dy_all, w_down_blk), 'tx', scatter_dimensi...  85.9 us
    reduce_scatter x1, waiting for transfers between devices, local_step(): lax.psum_scatter(jnp.dot(act_all, w_down_blk, preferred_element_type=jnp....  77.9 us
    reduce_scatter x1, waiting for transfers between devices, local_step(): lax.psum_scatter(contract_cols(d_gate_all, w_gate_blk) + contract_cols(d_...  74.4 us
    reduce_scatter x1, waiting for transfers between devices, local_step(): lax.psum_scatter(jnp.dot(h_all, w_up_blk, preferred_element_type=jnp.floa...  74.2 us
    all_gather x1, waiting for transfers between devices, local_step(): h_all = lax.all_gather(h_blk, 'ty', axis=0, tiled=True)  54 us
    all_gather x1, waiting for transfers between devices, local_step(): d_gate_all = lax.all_gather(d_gate, 'tx', axis=0, tiled=True)  38.9 us
    all_gather x1, waiting for transfers between devices, local_step(): dy_all = lax.all_gather(dy_blk, 'ty', axis=0, tiled=True)  35.6 us
  transfers between devices with their start and end apart: 10, of which 10 were waited for; matrix products, arithmetic and copies ran while one was open for 11% of the time, Pallas kernels for 0%

commit v1 on v0

v1 whole, which is shorter than its diff:
```python
import functools

import jax
import jax.numpy as jnp
from jax import lax
from jax.experimental import pallas as pl
from jax.experimental.pallas import tpu as pltpu
from jax.sharding import PartitionSpec as P

LN_EPS = 1e-6
MESH = pl.DeviceIdType.MESH
F32 = jnp.float32
BF16 = jnp.bfloat16
NZ = 4
NTY = 8
NTX = 4


def contract_rows(left_op, right_op):
    return lax.dot_general(left_op, right_op, (((0,), (0,)), ((), ())), preferred_element_type=F32)


def contract_cols(left_op, right_op):
    return lax.dot_general(left_op, right_op, (((1,), (1,)), ((), ())), preferred_element_type=F32)


def remote(src, dst, send_sem, recv_sem, device):
    return pltpu.make_async_remote_copy(src_ref=src, dst_ref=dst, send_sem=send_sem, recv_sem=recv_sem,
                                        device_id=device, device_id_type=MESH)


def gather_kernel(x_ref, dy_ref, gain_ref, w1_ref, w3_ref, w2_ref,
                  a_out, du_out, dv_out, hq_out, dyq_out, stat_out,
                  h_buf, dy_buf, w1f, w3f, w2f, u_buf, v_buf, a_buf, du_buf, dv_buf, st_src, st_buf,
                  st_s, st_r, x_s, x_r, up_s, dn_s, z_r, y_s, y_r, d_s, d_r, w_s, w_r, w_l, e_s, e_r, e_l, o_l):
    ty, tx = lax.axis_index("ty"), lax.axis_index("tx")
    z, y, core = ty // 2, ty % 2, tx % 2
    yp, up, dn = ty + 1 - 2 * y, ty + 2, ty - 2
    cp, xp, dp = tx + 1 - 2 * core, (tx + 2) % NTX, NTX - 1 - tx
    tb, dq = x_ref.shape
    d_model = dq * NTX
    fh = w1_ref.shape[1] // 2

    barrier = pltpu.get_barrier_semaphore()
    for dev in ((yp, tx), (ty, cp), (ty, xp), (ty, dp)):
        pl.semaphore_signal(barrier, inc=1, device_id=dev, device_id_type=MESH)

    @pl.when(z < NZ - 1)
    def _():
        pl.semaphore_signal(barrier, inc=1, device_id=(up, tx), device_id_type=MESH)

    @pl.when(z > 0)
    def _():
        pl.semaphore_signal(barrier, inc=1, device_id=(dn, tx), device_id_type=MESH)

    x_float = x_ref[...].astype(F32)
    lane = lax.broadcasted_iota(jnp.int32, (tb, 128), 1)
    sum_1 = jnp.sum(x_float, axis=1, keepdims=True)
    sum_2 = jnp.sum(x_float * x_float, axis=1, keepdims=True)
    packed = jnp.where(lane == 0, sum_1, jnp.where(lane == 1, sum_2, 0.0))
    st_src[...] = packed.T[:8]

    pl.semaphore_wait(barrier, 5 + z * (NZ - 1 - z) // 2)

    tx_peers = ((0, cp), (1, xp), (2, dp))
    bufs = (h_buf, dy_buf)

    def block(t, q, row_ty):
        return bufs[t].at[pl.ds(pl.multiple_of(row_ty * tb, tb), tb), pl.ds(pl.multiple_of(q * dq, dq), dq)]

    def quarter(s, q):
        return q if s == 0 else (q + 2) % NTX

    def stat_copy(r, dev):
        return remote(st_src, st_buf.at[r], st_s.at[r], st_r.at[r], (ty, dev))

    def x_copy(t):
        ref = block(t, tx, ty)
        return remote(ref, ref, x_s.at[t], x_r.at[t], (ty, xp))

    def x_arrive(t):
        ref = block(t, xp, ty)
        return remote(ref, ref, x_s.at[t], x_r.at[t], (ty, xp))

    def z_copy(t, s, layer, sem, dev):
        ref = block(t, quarter(s, tx), layer * 2 + y)
        return remote(ref, ref, sem.at[t, s, layer], z_r.at[t, s, layer], (dev, tx))

    def y_copy(t, s, layer, row_ty):
        ref = block(t, quarter(s, tx), row_ty)
        return remote(ref, ref, y_s.at[t, s, layer], y_r.at[t, s, layer], (yp, tx))

    def d_copy(t, s, row_ty, q):
        ref = block(t, quarter(s, q), row_ty)
        return remote(ref, ref, d_s.at[t, s, row_ty], d_r.at[t, s, row_ty], (ty, cp))

    def spread(t, s, layer):
        y_copy(t, s, layer, layer * 2 + y).start()
        d_copy(t, s, layer * 2 + y, tx).start()

    def send_own(t, s):
        @pl.when(z < NZ - 1)
        def _():
            z_copy(t, s, z, up_s, up).start()

        @pl.when(z > 0)
        def _():
            z_copy(t, s, z, dn_s, dn).start()

        spread(t, s, z)

    w_shards = (w1_ref, w3_ref, w2_ref)
    w_full = (w1f, w3f, w2f)

    def w_copy(w, r, dev):
        half = pl.ds(pl.multiple_of((dev % 2) * fh, fh), fh)
        mine = pl.ds(pl.multiple_of(tx * dq, dq), dq)
        src = w_shards[w].at[half, :] if w == 2 else w_shards[w].at[:, half]
        dst = w_full[w].at[:, mine] if w == 2 else w_full[w].at[mine, :]
        return remote(src, dst, w_s.at[w, r], w_r.at[w, r], (ty, dev))

    def w_arrive(w, r, dev):
        theirs = pl.ds(pl.multiple_of(dev * dq, dq), dq)
        dst = w_full[w].at[:, theirs] if w == 2 else w_full[w].at[theirs, :]
        return remote(dst, dst, w_s.at[w, r], w_r.at[w, r], (ty, dev))

    def w_local(w):
        half = pl.ds(pl.multiple_of(core * fh, fh), fh)
        mine = pl.ds(pl.multiple_of(tx * dq, dq), dq)
        src = w_shards[w].at[half, :] if w == 2 else w_shards[w].at[:, half]
        dst = w_full[w].at[:, mine] if w == 2 else w_full[w].at[mine, :]
        return pltpu.make_async_copy(src, dst, w_l.at[w])

    for r, dev in tx_peers:
        stat_copy(r, dev).start()
    own_rows = pl.ds(pl.multiple_of(ty * tb, tb), tb)
    own_cols = pl.ds(pl.multiple_of(tx * dq, dq), dq)
    dy_buf[own_rows, own_cols] = dy_ref[...]
    for w in range(3):
        w_local(w).start()
        w_copy(w, 0, cp).start()
    x_copy(1).start()
    send_own(1, 0)
    for r, dev in tx_peers:
        stat_copy(r, dev).wait_recv()
    total = st_src[...] + st_buf[0] + st_buf[1] + st_buf[2]
    total = jnp.concatenate([total, jnp.zeros((120, tb), F32)], axis=0).T
    mean_x = total[:, 0:1] / d_model
    inv_std = lax.rsqrt(total[:, 1:2] / d_model - mean_x * mean_x + LN_EPS)
    x_hat = (x_float - mean_x) * inv_std
    h_buf[own_rows, own_cols] = (gain_ref[...] * x_hat).astype(BF16)
    stat_out[...] = jnp.where(lane == 0, mean_x, jnp.where(lane == 1, inv_std, 0.0))
    x_copy(0).start()
    send_own(0, 0)
    for w in range(3):
        w_copy(w, 1, xp).start()
        w_copy(w, 2, dp).start()

    for t in (1, 0):
        x_arrive(t).wait_recv()
        send_own(t, 1)
    order = ((1, 0), (0, 0), (1, 1), (0, 1))
    for k in range(1, NZ):
        for t, s in order:
            @pl.when(z >= k)
            def _():
                layer = z - k
                z_copy(t, s, layer, up_s, dn).wait_recv()

                @pl.when(z < NZ - 1)
                def _():
                    z_copy(t, s, layer, up_s, up).start()

                spread(t, s, layer)

            @pl.when(z + k < NZ)
            def _():
                layer = z + k
                z_copy(t, s, layer, dn_s, up).wait_recv()

                @pl.when(z > 0)
                def _():
                    z_copy(t, s, layer, dn_s, dn).start()

                spread(t, s, layer)

    def wait_w(w):
        w_local(w).wait()
        for r, dev in tx_peers:
            w_arrive(w, r, dev).wait_recv()

    def up_proj(row_ty):
        rows = pl.ds(pl.multiple_of(row_ty * tb, tb), tb)
        for s in (0, 1):
            d_copy(0, s, row_ty, cp).wait_recv()
        h_rows = h_buf[rows, :]
        u_buf[rows, :] = jnp.dot(h_rows, w1f[...], preferred_element_type=F32)
        v_buf[rows, :] = jnp.dot(h_rows, w3f[...], preferred_element_type=F32)

    wait_w(0)
    wait_w(1)

    def own_y(n, _):
        up_proj(n * 2 + y)
        return 0

    def other_y(n, _):
        row_ty = n * 2 + 1 - y
        for t, s in order:
            y_copy(t, s, n, row_ty).wait_recv()
            d_copy(t, s, row_ty, tx).start()
        up_proj(row_ty)
        return 0

    lax.fori_loop(0, NZ, own_y, 0)
    lax.fori_loop(0, NZ, other_y, 0)

    hq_copy = pltpu.make_async_copy(h_buf.at[:, own_cols], hq_out, o_l.at[0])
    dyq_copy = pltpu.make_async_copy(dy_buf.at[:, own_cols], dyq_out, o_l.at[1])
    hq_copy.start()
    dyq_copy.start()
    wait_w(2)

    res_bufs = (a_buf, du_buf, dv_buf)
    res_outs = (a_out, du_out, dv_out)

    def e_copy(i, row_ty, c):
        rows = pl.ds(pl.multiple_of(row_ty * tb, tb), tb)
        cols = pl.ds(pl.multiple_of(c * fh, fh), fh)
        return remote(res_bufs[i].at[rows, :], res_outs[i].at[rows, cols], e_s.at[i, row_ty], e_r.at[i, row_ty],
                      (ty, cp))

    def e_local(i, row_ty):
        rows = pl.ds(pl.multiple_of(row_ty * tb, tb), tb)
        cols = pl.ds(pl.multiple_of(core * fh, fh), fh)
        return pltpu.make_async_copy(res_bufs[i].at[rows, :], res_outs[i].at[rows, cols], e_l.at[i, row_ty])

    def down_proj(row_ty, _):
        rows = pl.ds(pl.multiple_of(row_ty * tb, tb), tb)
        for s in (0, 1):
            d_copy(1, s, row_ty, cp).wait_recv()
        d_act = contract_cols(dy_buf[rows, :], w2f[...])
        gate, up_v = u_buf[rows, :], v_buf[rows, :]
        sig = jax.nn.sigmoid(gate)
        swish = gate * sig
        a_buf[rows, :] = (swish * up_v).astype(BF16)
        du_buf[rows, :] = (d_act * up_v * sig * (1.0 + gate * (1.0 - sig))).astype(BF16)
        dv_buf[rows, :] = (d_act * swish).astype(BF16)

        @pl.when(row_ty > 0)
        def _():
            for i in range(3):
                e_copy(i, row_ty - 1, core).start()
                e_local(i, row_ty - 1).start()

        return 0

    lax.fori_loop(0, NTY, down_proj, 0)
    for i in range(3):
        e_copy(i, NTY - 1, core).start()
        e_local(i, NTY - 1).start()

    for r, dev in tx_peers:
        stat_copy(r, dev).wait_send()
        for w in range(3):
            w_copy(w, r, dev).wait_send()
    for t in (0, 1):
        x_copy(t).wait_send()

    def drain(layer, _):
        for t, s in order:
            @pl.when(jnp.logical_and(z < NZ - 1, layer <= z))
            def _():
                z_copy(t, s, layer, up_s, up).wait_send()

            @pl.when(jnp.logical_and(z > 0, layer >= z))
            def _():
                z_copy(t, s, layer, dn_s, dn).wait_send()

            y_copy(t, s, layer, layer * 2 + y).wait_send()
            d_copy(t, s, layer * 2, tx).wait_send()
            d_copy(t, s, layer * 2 + 1, tx).wait_send()
        return 0

    lax.fori_loop(0, NZ, drain, 0)

    def drain_e(row_ty, _):
        for i in range(3):
            e_copy(i, row_ty, core).wait_send()
            e_copy(i, row_ty, 1 - core).wait_recv()
            e_local(i, row_ty).wait()
        return 0

    lax.fori_loop(0, NTY, drain_e, 0)
    hq_copy.wait()
    dyq_copy.wait()


def gather_step(x_blk, dy_blk, gain_blk, w1, w3, w2):
    tb, dq = x_blk.shape
    tokens, d_model, f_loc = tb * NTY, dq * NTX, w1.shape[1]
    fh = f_loc // 2
    dma = pltpu.SemaphoreType.DMA
    vmem = pl.BlockSpec(memory_space=pltpu.VMEM)
    hbm = pl.BlockSpec(memory_space=pl.ANY)
    return pl.pallas_call(
        gather_kernel,
        out_shape=(
            [jax.ShapeDtypeStruct((tokens, f_loc), BF16)] * 3
            + [jax.ShapeDtypeStruct((tokens, dq), BF16)] * 2
            + [jax.ShapeDtypeStruct((tb, 128), F32)]),
        in_specs=[vmem, vmem, vmem, hbm, hbm, hbm],
        out_specs=[hbm] * 5 + [vmem],
        scratch_shapes=[
            pltpu.VMEM((tokens, d_model), BF16), pltpu.VMEM((tokens, d_model), BF16),
            pltpu.VMEM((d_model, fh), BF16), pltpu.VMEM((d_model, fh), BF16), pltpu.VMEM((fh, d_model), BF16),
            pltpu.VMEM((tokens, fh), F32), pltpu.VMEM((tokens, fh), F32),
            pltpu.VMEM((tokens, fh), BF16), pltpu.VMEM((tokens, fh), BF16), pltpu.VMEM((tokens, fh), BF16),
            pltpu.VMEM((8, tb), F32), pltpu.VMEM((3, 8, tb), F32),
            dma((3,)), dma((3,)), dma((2,)), dma((2,)),
            dma((2, 2, NZ)), dma((2, 2, NZ)), dma((2, 2, NZ)), dma((2, 2, NZ)), dma((2, 2, NZ)),
            dma((2, 2, NTY)), dma((2, 2, NTY)),
            dma((3, 3)), dma((3, 3)), dma((3,)),
            dma((3, NTY)), dma((3, NTY)), dma((3, NTY)), dma((2,)),
        ],
        compiler_params=pltpu.CompilerParams(collective_id=0, has_side_effects=True,
                                             vmem_limit_bytes=66_000_000),
        cost_estimate=pl.CostEstimate(flops=6 * tokens * d_model * fh, bytes_accessed=40_000_000,
                                      transcendentals=tokens * fh),
    )(x_blk, dy_blk, gain_blk, w1, w3, w2)


def solution(mesh):
    tx_size = mesh.shape["tx"]

    def local_step(x_blk, dy_blk, gain_blk, w_gate_blk, w_up_blk, w_down_blk):
        d_model = x_blk.shape[1] * tx_size
        gain_row = gain_blk[None, :]
        act_all, d_gate_all, d_up_all, h_all, dy_all, stats = gather_step(
            x_blk, dy_blk, gain_row, w_gate_blk, w_up_blk, w_down_blk)
        x_float = x_blk.astype(F32)
        mean_x, inv_std = stats[:, 0:1], stats[:, 1:2]
        x_hat = (x_float - mean_x) * inv_std
        mlp_out = lax.psum_scatter(jnp.dot(act_all, w_down_blk, preferred_element_type=F32),
                                   "ty", scatter_dimension=0, tiled=True)
        y_blk = (x_float + mlp_out).astype(BF16)
        dw_down_blk = contract_rows(act_all, dy_all)
        dw_gate_blk = contract_rows(h_all, d_gate_all)
        dw_up_blk = contract_rows(h_all, d_up_all)
        d_hnorm = lax.psum_scatter(contract_cols(d_gate_all, w_gate_blk) + contract_cols(d_up_all, w_up_blk),
                                   "ty", scatter_dimension=0, tiled=True)
        d_xhat = d_hnorm * gain_blk
        bwd_stats = lax.psum(jnp.stack([jnp.sum(d_xhat, axis=1), jnp.sum(d_xhat * x_hat, axis=1)]), "tx") / d_model
        dx_ln = inv_std * (d_xhat - bwd_stats[0][:, None] - x_hat * bwd_stats[1][:, None])
        dx_blk = (dy_blk.astype(F32) + dx_ln).astype(BF16)
        d_gain_blk = lax.psum(jnp.sum(d_hnorm * x_hat, axis=0), "ty")
        return (y_blk, dx_blk, dw_gate_blk, dw_up_blk, dw_down_blk, d_gain_blk)

    return jax.shard_map(
        local_step, mesh=mesh,
        in_specs=(P("ty", "tx"), P("ty", "tx"), P("tx"), P("tx", "ty"), P("tx", "ty"), P("ty", "tx")),
        out_specs=(P("ty", "tx"), P("ty", "tx"), P("tx", "ty"), P("tx", "ty"), P("ty", "tx"), P("tx")),
        check_vma=False)
```

time: 748 us -> 395 us (0.53)
  waiting for transfers between devices: 593 us -> 158 us
  Pallas kernels: 0 us -> 143 us
  matrix products: 82.3 us -> 44.3 us
  other arithmetic: 13.9 us -> 3.88 us
  blocking collectives: 35.3 us -> 26.9 us
    reduce_scatter x4 -> x1, waiting for transfers between devices: 324 us -> 77.9 us  [local_step(): lax.psum_scatter(jnp.dot(act_all, w_down_blk, preferred_element_type=F32)...]
    all_gather x5 -> x0, waiting for transfers between devices: 193 us -> none  [the longest x1 54 us: local_step(): h_all = lax.all_gather(h_blk, 'ty', axis=0, tiled=True)]
    pallas_call x0 -> x1, Pallas kernels: none -> 143 us  [gather_step(): pl.pallas_call(gather_kernel, out_shape=[jax.ShapeDtypeStruct((tokens, f_...]
    dot_general x3 -> x1, matrix products: 28.6 us -> 9.07 us  [local_step(): jnp.dot(act_all, w_down_blk, preferred_element_type=F32)]
    dot_general x3 -> x2, matrix products: 30.7 us -> 12.8 us  [contract_cols(): lax.dot_general(left_op, right_op, (((1,), (1,)), ((), ())), preferred_el...]
    convert_element_type x3 -> x1, other arithmetic: 11.1 us -> 2.4 us  [local_step(): dx_blk = (dy_blk.astype(F32) + dx_ln).astype(BF16)]
    psum x2 -> x1, blocking collectives: 14.5 us -> 6.04 us  [local_step(): lax.psum(jnp.stack([jnp.sum(d_xhat, axis=1), jnp.sum(d_xhat * x_hat, axis...]
  transfers between devices with their start and end apart: 10 -> 2, of which waited for: 10 -> 2; matrix products, arithmetic and copies ran while one was open for 11% -> 8% of each run, Pallas kernels for 0% -> 0%
where the time goes in v1:
time: 395 us
  waiting for transfers between devices  158 us (40%)
  Pallas kernels  143 us (36%)
  matrix products  44.3 us (11%)
  blocking collectives  26.9 us (7%)
  between operations  14.1 us (4%)
  local copies, waits for them, and re-layouts  4.28 us (1%)
    pallas_call x1, Pallas kernels, gather_step(): pl.pallas_call(gather_kernel, out_shape=[jax.ShapeDtypeStruct((tokens, f_...  143 us
    reduce_scatter x1, waiting for transfers between devices, local_step(): lax.psum_scatter(contract_cols(d_gate_all, w_gate_blk) + contract_cols(d_...  80.2 us
    reduce_scatter x1, waiting for transfers between devices, local_step(): lax.psum_scatter(jnp.dot(act_all, w_down_blk, preferred_element_type=F32)...  77.9 us
    dot_general x3, matrix products, contract_rows(): lax.dot_general(left_op, right_op, (((0,), (0,)), ((), ())), preferred_el...  22.4 us
    psum x1, blocking collectives, local_step(): d_gain_blk = lax.psum(jnp.sum(d_hnorm * x_hat, axis=0), 'ty')  20.8 us
    dot_general x2, matrix products, contract_cols(): lax.dot_general(left_op, right_op, (((1,), (1,)), ((), ())), preferred_el...  12.8 us
    dot_general x1, matrix products, local_step(): jnp.dot(act_all, w_down_blk, preferred_element_type=F32)  9.07 us
  transfers between devices with their start and end apart: 2, of which 2 were waited for; matrix products, arithmetic and copies ran while one was open for 8% of the time, Pallas kernels for 0%

profile of v1, /device:TPU:0, one launch (start us, length us, event | category | flops | bytes accessed | tf_op | source)
XLA Modules:
  0.0 394.8 jit_solution(8129633637508165201)
XLA Ops:
  7.2 0.0 reduce-scatter.5.cloned.1.call-start
  7.2 1.3 broadcast_in_dim.4.gain_ref
  8.5 143.0 %shard_map.109 = (bf16[2048,1280]{1,0:T(8,128)(2,1)}, bf16[2048,1280]{1,0:T(8,128)(2,1)}, bf16[2048,1280]{1,0:T(8,128)(2,1)}, bf16[2048,640]{1,0:T(8,128)(2,1)},...) custom-call(bf16[256,640]{1,0:T(8,128)(2,1)} %x_ref.1, bf16[256,640]{1,0:T(8,128)(2,1)} %dy_ref.1, ...), custom_call_target="tpu_custom_call" | custom-call | flops 20132659200 | bytes 40000000 | tf_op jit(solution)/shard_map/pallas_call | solution.py:306
  151.4 0.0 copy-start.4
  151.5 0.0 copy-start.7
  151.5 6.9 %fusion.13 = f32[2048,640]{1,0:T(8,128)S(1)} fusion(bf16[2048,1280]{1,0:T(8,128)(2,1)} %get-tuple-element.14, bf16[640,1280]{1,0:T(8,128)(2,1)} %w1_ref.1), kind=kOutput, calls=%fused_computation.21 | convolution fusion | flops 3355443200 | bytes 12124160 | tf_op jit(solution)/shard_map/dot_general | solution.py:24
  158.3 0.0 copy-done.4
  158.3 0.0 copy-done.7
  158.4 6.0 %convolution_add_fusion = f32[2048,640]{1,0:T(8,128)} fusion(f32[2048,640]{1,0:T(8,128)S(1)} %fusion.13, bf16[2048,1280]{1,0:T(8,128)(2,1)S(1)} %copy-done.7, bf16[640,1280]{1,0:T(8,128)(2,1)S(1)} %copy-done.4), kind=kOutput, calls=%fused_computation | convolution fusion | flops 3356753920 | bytes 17367040 | tf_op jit(solution)/shard_map/dot_general | solution.py:24
  164.3 0.0 copy-start.5
  164.3 0.0 reduce-scatter.5.cloned.1.call-update
  164.4 0.2 reduce-scatter.3.cloned.1.call-start
  164.6 1.2 copy-done.5
  165.8 9.1 %fusion.12 = f32[2048,640]{1,0:T(8,128)} fusion(bf16[2048,1280]{1,0:T(8,128)(2,1)} %get-tuple-element.12, bf16[1280,640]{1,0:T(8,128)(2,1)S(1)} %copy-done.5), kind=kOutput, calls=%fused_computation.20 | convolution fusion | flops 3355443200 | bytes 12124160 | tf_op jit(solution)/shard_map/dot_general | solution.py:344
  174.8 0.0 copy-start.1
  174.8 0.0 copy-start.8
  174.8 0.0 reduce-scatter.3.cloned.1.call-update
  174.9 0.9 copy-done.1
  175.7 0.2 slice_reduce_fusion.1
  176.0 0.7 copy-done.8
  176.7 0.0 slice-start
  176.7 8.0 %fusion.14 = f32[640,1280]{1,0:T(8,128)} fusion(bf16[2048,640]{1,0:T(8,128)(2,1)S(1)} %copy-done.8, bf16[2048,1280]{1,0:T(8,128)(2,1)} %get-tuple-element.14), kind=kOutput, calls=%fused_computation.22 | convolution fusion | flops 3355443200 | bytes 11141120 | tf_op jit(solution)/shard_map/dot_general | solution.py:20
  184.7 0.0 slice-start.1
  184.7 0.0 copy-start.6
  184.7 8.0 %fusion.15 = f32[640,1280]{1,0:T(8,128)} fusion(bf16[2048,640]{1,0:T(8,128)(2,1)S(1)} %copy-done.8, bf16[2048,1280]{1,0:T(8,128)(2,1)} %get-tuple-element.15), kind=kOutput, calls=%fused_computation.23 | convolution fusion | flops 3355443200 | bytes 11141120 | tf_op jit(solution)/shard_map/dot_general | solution.py:20
  192.7 0.0 slice-done
  192.7 0.0 slice-done.1
  192.7 0.0 copy-done.6
  192.7 0.0 copy-start
  192.7 0.0 copy-start.3
  192.7 0.0 copy-start.2
  192.7 6.4 %fusion.16 = f32[1280,640]{1,0:T(8,128)} fusion(bf16[2048,1280]{1,0:T(8,128)(2,1)S(1)} %bitcast.21, bf16[2048,640]{1,0:T(8,128)(2,1)S(1)} %copy-done.6), kind=kOutput, calls=%fused_computation.24 | convolution fusion | flops 3355443200 | bytes 11141120 | tf_op jit(solution)/shard_map/dot_general | solution.py:20
  199.1 80.2 %reduce-scatter.5.cloned.1.call-done = f32[256,640]{1,0:T(8,128)} async-done(((f32[2048,640]{1,0:T(8,128)}), f32[256,640]{1,0:T(8,128)}) %reduce-scatter.5.cloned.1.call-update) | async-done | bytes 655376 | tf_op jit(solution)/shard_map/reduce_scatter | solution.py:350
  279.3 0.0 copy-done
  279.3 0.0 copy-done.3
  279.3 1.5 fusion.10
  280.8 20.8 %psum.15 = f32[640]{0:T(1024)} all-reduce(f32[640]{0:T(1024)S(1)} %get-tuple-element.18), channel_id=1, replica_groups=mesh['ty'=8,'tx'=4] {'ty'}, use_global_device_ids=true, to_apply=%region_6.0 | all-reduce | flops 640 | bytes 5120 | tf_op jit(solution)/shard_map/psum | solution.py:356
  301.6 6.0 %psum.14 = f32[2,256]{1,0:T(2,128)S(1)} all-reduce(f32[2,256]{1,0:T(2,128)S(1)} %pad_maximum_fusion), channel_id=1, replica_groups=mesh['ty'=8,'tx'=4] {'tx'}, use_global_device_ids=true, to_apply=%region_4.0 | all-reduce | flops 512 | bytes 4096 | tf_op jit(solution)/shard_map/psum | solution.py:353
  307.6 77.9 %reduce-scatter.3.cloned.1.call-done = f32[256,640]{1,0:T(8,128)} async-done(((f32[2048,640]{1,0:T(8,128)}), f32[256,640]{1,0:T(8,128)}) %reduce-scatter.3.cloned.1.call-update) | async-done | bytes 655376 | tf_op jit(solution)/shard_map/reduce_scatter | solution.py:344
  385.6 0.0 copy-done.2
  385.6 2.4 fusion.9
  (4 shorter events, 0.0 us)
Async XLA Ops:
  7.2 272.1 %reduce-scatter.5.cloned.1.call-start = ((), (), s32[]{:S(2)}) async-start(), calls=%async_computation.3 | async-start | bytes 5898240 | tf_op jit(solution)/shard_map/reduce_scatter | solution.py:350
  151.4 6.9 %copy-start.4 = (bf16[640,1280]{1,0:T(8,128)(2,1)S(1)}, bf16[640,1280]{1,0:T(8,128)(2,1)}, u32[]{:S(2)}) copy-start(bf16[640,1280]{1,0:T(8,128)(2,1)} %w3_ref.1) | copy-start | bytes 4915204
  151.5 6.9 %copy-start.7 = (bf16[2048,1280]{1,0:T(8,128)(2,1)S(1)}, bf16[2048,1280]{1,0:T(8,128)(2,1)}, u32[]{:S(2)}) copy-start(bf16[2048,1280]{1,0:T(8,128)(2,1)} %get-tuple-element.15) | copy-start | bytes 15728644
  164.3 1.4 copy-start.5
  164.4 221.2 %reduce-scatter.3.cloned.1.call-start = ((), (), s32[]{:S(2)}) async-start(), calls=%async_computation.2 | async-start | bytes 5898240 | tf_op jit(solution)/shard_map/reduce_scatter | solution.py:344
  174.8 0.9 copy-start.1
  174.8 1.8 copy-start.8
  176.7 16.0 %slice-start = ((s8[5242880]{0:T(1024)(128)(4,1)}), s8[4194304]{0:T(1024)(128)(4,1)S(1)}, s32[]{:S(2)}) async-start(s8[5242880]{0:T(1024)(128)(4,1)} %bitcast.20), calls=%async_computation.4 | async-start | bytes 8388608
  184.7 8.0 %slice-start.1 = ((s8[5242880]{0:T(1024)(128)(4,1)}), s8[1048576]{0:T(1024)(128)(4,1)S(1)}, s32[]{:S(2)}) async-start(s8[5242880]{0:T(1024)(128)(4,1)} %bitcast.20), calls=%async_computation.5 | async-start | bytes 2097152
  184.7 8.0 %copy-start.6 = (bf16[2048,640]{1,0:T(8,128)(2,1)S(1)}, bf16[2048,640]{1,0:T(8,128)(2,1)}, u32[]{:S(2)}) copy-start(bf16[2048,640]{1,0:T(8,128)(2,1)} %get-tuple-element.17) | copy-start | bytes 7864324
  192.7 86.6 %copy-start = (bf16[256,640]{1,0:T(8,128)(2,1)S(1)}, bf16[256,640]{1,0:T(8,128)(2,1)}, u32[]{:S(2)}) copy-start(bf16[256,640]{1,0:T(8,128)(2,1)} %x_ref.1) | copy-start | bytes 983044
  192.7 86.6 %copy-start.3 = (f32[640]{0:T(1024)S(1)}, f32[640]{0:T(1024)}, u32[]{:S(2)}) copy-start(f32[640]{0:T(1024)} %param.8) | copy-start | bytes 7684
  192.7 192.8 %copy-start.2 = (bf16[256,640]{1,0:T(8,128)(2,1)S(1)}, bf16[256,640]{1,0:T(8,128)(2,1)}, u32[]{:S(2)}) copy-start(bf16[256,640]{1,0:T(8,128)(2,1)} %dy_ref.1) | copy-start | bytes 983044
Sparse Core Ops, SparseCore 0:
  164.5 114.7 reduce-scatter.4
  282.9 102.6 reduce-scatter.2

commit v2 on v1

--- a/solution.py
+++ b/solution.py
@@ -14,6 +14,9 @@
 NZ = 4
 NTY = 8
 NTX = 4
+SUB = 64
+SUBS = 4
+LAG = 2
 
 
 def contract_rows(left_op, right_op):
@@ -330,31 +333,308 @@
     )(x_blk, dy_blk, gain_blk, w1, w3, w2)
 
 
+def scatter_kernel(x_ref, dy_ref, gain_ref, stat_ref, a_in, du_in, dv_in, hq_in, dyq_in, w1_in, w3_in, w2_in,
+                   y_out, dx_out, dw1_out, dw3_out, dw2_out, dg_out,
+                   a_all, du_all, dv_all, hq, dyq, w1, w3, w2, y_send, y_recv, own, z_buf, z_fin,
+                   dw1_st, dw3_st, dw2_st, pack, sb_src, sb_buf, dg_buf,
+                   in_l, y_s, y_r, z_s, z_r, f_r, dw_l, sb_s, sb_r, dg_s, dg_r):
+    ty, tx = lax.axis_index("ty"), lax.axis_index("tx")
+    z, y, core = ty // 2, ty % 2, tx % 2
+    yp, up, dn = ty + 1 - 2 * y, ty + 2, ty - 2
+    cp, xp, dp = tx + 1 - 2 * core, (tx + 2) % NTX, NTX - 1 - tx
+    tx_peers = ((0, cp), (1, xp), (2, dp))
+    tb, dq = x_ref.shape
+    d_model = dq * NTX
+    f_loc = w1.shape[1]
+    far = z // 2 * z + (1 - z // 2) * (NZ - 1 - z)
+
+    loads = []
+    for n, (src, dst) in enumerate(((a_in, a_all), (w2_in, w2), (du_in, du_all), (dv_in, dv_all), (w1_in, w1),
+                                    (w3_in, w3), (dyq_in, dyq), (hq_in, hq))):
+        copy = pltpu.make_async_copy(src, dst, in_l.at[n])
+        copy.start()
+        loads.append(copy)
+
+    barrier = pltpu.get_barrier_semaphore()
+    for _, dev in tx_peers:
+        pl.semaphore_signal(barrier, inc=1, device_id=(ty, dev), device_id_type=MESH)
+    for r in range(1, NTY):
+        pl.semaphore_signal(barrier, inc=1, device_id=((ty + r) % NTY, tx), device_id_type=MESH)
+    pl.semaphore_wait(barrier, NTY + NTX - 2)
+
+    def where_of(i):
+        return i // (NZ * SUBS), 3 * (i % (NZ * SUBS) // SUBS) % NZ, i % SUBS
+
+    def sub_rows(sub):
+        return pl.ds(pl.multiple_of(sub * SUB, SUB), SUB)
+
+    def y_copy(i):
+        mat, layer, sub = where_of(i)
+        return remote(y_send.at[mat, layer, sub_rows(sub), :], y_recv.at[mat, layer, sub_rows(sub), :],
+                      y_s.at[i], y_r.at[i], (yp, tx))
+
+    def partial(mat, row_ty):
+        rows = pl.ds(pl.multiple_of(row_ty * tb, tb), tb)
+        if mat == 0:
+            return jnp.dot(a_all[rows, :], w2[...], preferred_element_type=F32)
+        return contract_cols(du_all[rows, :], w1[...]) + contract_cols(dv_all[rows, :], w3[...])
+
+    def send_block(mat, j):
+        for sub in range(SUBS):
+            y_copy((mat * NZ + j) * SUBS + sub).start()
+
+    def partner_rows(mat):
+        def step(j, _):
+            layer = 3 * j % NZ
+            y_send[mat, layer] = partial(mat, layer * 2 + 1 - y)
+
+            @pl.when(j > 0)
+            def _():
+                send_block(mat, j - 1)
+
+            return 0
+
+        lax.fori_loop(0, NZ, step, 0)
+        send_block(mat, NZ - 1)
+
+    def own_rows(mat):
+        def step(layer, _):
+            own[mat, layer] = partial(mat, layer * 2 + y)
+            return 0
+
+        lax.fori_loop(0, NZ, step, 0)
+
+    loads[0].wait()
+    loads[1].wait()
+    partner_rows(0)
+    for n in range(2, 6):
+        loads[n].wait()
+    partner_rows(1)
+    own_rows(0)
+    own_rows(1)
+    loads[6].wait()
+    loads[7].wait()
+
+    x_float = x_ref[...].astype(F32)
+    mean_x, inv_std = stat_ref[:, 0:1], stat_ref[:, 1:2]
+    dg_row = pl.ds(pl.multiple_of(ty * 8, 8), 8)
+    dg_buf[dg_row, :] = jnp.zeros((8, dq), F32)
+    pack[...] = jnp.zeros(pack.shape, F32)
+
+    def z_copy_up(i):
+        mat, layer, sub = where_of(i)
+        return remote(own.at[mat, layer, sub_rows(sub), :], z_buf.at[i], z_s.at[i], z_r.at[i], (up, tx))
+
+    def z_copy_dn(i):
+        mat, layer, sub = where_of(i)
+        return remote(own.at[mat, layer, sub_rows(sub), :], z_buf.at[i], z_s.at[i], z_r.at[i], (dn, tx))
+
+    def z_copy_fin(i):
+        mat, layer, sub = where_of(i)
+        k = mat * SUBS + sub
+        return remote(own.at[mat, layer, sub_rows(sub), :], z_fin.at[k], z_s.at[i], f_r.at[k], (dn, tx))
+
+    def add_run(i):
+        mat, layer, sub = where_of(i)
+        z_copy_up(i).wait_recv()
+        own[mat, layer, sub_rows(sub), :] = own[mat, layer, sub_rows(sub), :] + z_buf[i]
+
+    n_items = 2 * NZ * SUBS
+    chunk = 256
+    n_chunks = f_loc // chunk
+
+    def dw_copy(w, c):
+        cols = pl.ds(pl.multiple_of(c * chunk, chunk), chunk)
+        if w == 2:
+            return pltpu.make_async_copy(dw2_st.at[cols, :], dw2_out.at[cols, :], dw_l.at[w, c])
+        src, dst = ((dw1_st, dw1_out), (dw3_st, dw3_out))[w]
+        return pltpu.make_async_copy(src.at[:, cols], dst.at[:, cols], dw_l.at[w, c])
+
+    def weight_grads(slot):
+        for w in (2, 0, 1):
+            first = {2: 0, 0: n_chunks, 1: 2 * n_chunks}[w]
+
+            @pl.when(jnp.logical_and(slot >= first, slot < first + n_chunks))
+            def _():
+                c = slot - first
+                cols = pl.ds(pl.multiple_of(c * chunk, chunk), chunk)
+                if w == 2:
+                    dw2_st[cols, :] = contract_rows(a_all[:, cols], dyq[...])
+                elif w == 0:
+                    dw1_st[:, cols] = contract_rows(hq[...], du_all[:, cols])
+                else:
+                    dw3_st[:, cols] = contract_rows(hq[...], dv_all[:, cols])
+                dw_copy(w, c).start()
+
+    def slot_step(slot, _):
+        weight_grads(slot)
+
+        @pl.when(slot < n_items)
+        def _():
+            mat, layer, sub = where_of(slot)
+            y_copy(slot).wait_recv()
+            own[mat, layer, sub_rows(sub), :] = (own[mat, layer, sub_rows(sub), :]
+                                                 + y_recv[mat, layer, sub_rows(sub), :])
+
+        i_up = slot - LAG * z
+        l_up = where_of(jnp.maximum(i_up, 0))[1]
+
+        @pl.when(jnp.logical_and(jnp.logical_and(i_up >= 0, i_up < n_items), l_up > z))
+        def _():
+            @pl.when(z > 0)
+            def _():
+                add_run(i_up)
+
+            z_copy_up(i_up).start()
+
+        i_dn = slot - LAG * (NZ - 1 - z)
+        l_dn = where_of(jnp.maximum(i_dn, 0))[1]
+
+        @pl.when(jnp.logical_and(jnp.logical_and(i_dn >= 0, i_dn < n_items), l_dn < z))
+        def _():
+            @pl.when(z < NZ - 1)
+            def _():
+                add_run(i_dn)
+
+            @pl.when(l_dn < z - 1)
+            def _():
+                z_copy_dn(i_dn).start()
+
+            @pl.when(l_dn == z - 1)
+            def _():
+                z_copy_fin(i_dn).start()
+
+        i_fin = slot - LAG * far
+        l_fin = where_of(jnp.maximum(i_fin, 0))[1]
+
+        @pl.when(jnp.logical_and(jnp.logical_and(i_fin >= 0, i_fin < n_items), l_fin == z))
+        def _():
+            mat, layer, sub = where_of(i_fin)
+
+            @pl.when(z > 0)
+            def _():
+                add_run(i_fin)
+
+            @pl.when(z < NZ - 1)
+            def _():
+                z_copy_fin(i_fin).wait_recv()
+                own[mat, layer, sub_rows(sub), :] = own[mat, layer, sub_rows(sub), :] + z_fin[mat * SUBS + sub]
+
+            rows = sub_rows(sub)
+
+            @pl.when(mat == 0)
+            def _():
+                y_out[rows, :] = (x_ref[rows, :].astype(F32) + own[0, layer, rows, :]).astype(BF16)
+
+            @pl.when(mat == 1)
+            def _():
+                d_h = own[1, layer, rows, :]
+                x_hat = (x_ref[rows, :].astype(F32) - stat_ref[rows, 0:1]) * stat_ref[rows, 1:2]
+                d_xhat = d_h * gain_ref[...]
+                lane = lax.broadcasted_iota(jnp.int32, (SUB, 128), 1)
+                pack[rows, :] = jnp.where(lane == 0, jnp.sum(d_xhat, axis=1, keepdims=True),
+                                          jnp.where(lane == 1, jnp.sum(d_xhat * x_hat, axis=1, keepdims=True), 0.0))
+                dg_buf[dg_row, :] = dg_buf[dg_row, :] + jnp.sum((d_h * x_hat).reshape(SUB // 8, 8, dq), axis=0)
+
+        return 0
+
+    lax.fori_loop(0, n_items + LAG * (NZ - 2), slot_step, 0)
+
+    def dg_copy(r, row):
+        ref = dg_buf.at[pl.ds(pl.multiple_of(row * 8, 8), 8), :]
+        return remote(ref, ref, dg_s.at[r], dg_r.at[row], ((ty + r) % NTY, tx))
+
+    def sb_copy(r, dev):
+        return remote(sb_src, sb_buf.at[r], sb_s.at[r], sb_r.at[r], (ty, dev))
+
+    sb_src[...] = pack[...].T[:8]
+    for r in range(1, NTY):
+        dg_copy(r, ty).start()
+    for r, dev in tx_peers:
+        sb_copy(r, dev).start()
+    x_hat = (x_float - mean_x) * inv_std
+    d_xhat = own[1, z] * gain_ref[...]
+    for r, dev in tx_peers:
+        sb_copy(r, dev).wait_recv()
+    total = sb_src[...] + sb_buf[0] + sb_buf[1] + sb_buf[2]
+    total = jnp.concatenate([total, jnp.zeros((120, tb), F32)], axis=0).T / d_model
+    dx_ln = inv_std * (d_xhat - total[:, 0:1] - x_hat * total[:, 1:2])
+    dx_out[...] = (dy_ref[...].astype(F32) + dx_ln).astype(BF16)
+    for r in range(1, NTY):
+        dg_copy(r, (ty + NTY - r) % NTY).wait_recv()
+    dg_out[...] = jnp.sum(dg_buf[...], axis=0, keepdims=True)
+
+    for r in range(1, NTY):
+        dg_copy(r, ty).wait_send()
+    for r, dev in tx_peers:
+        sb_copy(r, dev).wait_send()
+
+    def drain(i, _):
+        y_copy(i).wait_send()
+        layer = where_of(i)[1]
+
+        @pl.when(layer > z)
+        def _():
+            z_copy_up(i).wait_send()
+
+        @pl.when(layer < z)
+        def _():
+            z_copy_dn(i).wait_send()
+
+        return 0
+
+    lax.fori_loop(0, n_items, drain, 0)
+
+    def drain_dw(c, _):
+        for w in range(3):
+            dw_copy(w, c).wait()
+        return 0
+
+    lax.fori_loop(0, n_chunks, drain_dw, 0)
+
+
+def scatter_step(x_blk, dy_blk, gain_row, stats, act_all, d_gate_all, d_up_all, hq, dyq, w1, w3, w2):
+    tb, dq = x_blk.shape
+    tokens, f_loc = tb * NTY, w1.shape[1]
+    dma = pltpu.SemaphoreType.DMA
+    vmem = pl.BlockSpec(memory_space=pltpu.VMEM)
+    hbm = pl.BlockSpec(memory_space=pl.ANY)
+    items = 2 * NZ * SUBS
+    return pl.pallas_call(
+        scatter_kernel,
+        out_shape=[
+            jax.ShapeDtypeStruct((tb, dq), BF16), jax.ShapeDtypeStruct((tb, dq), BF16),
+            jax.ShapeDtypeStruct((dq, f_loc), F32), jax.ShapeDtypeStruct((dq, f_loc), F32),
+            jax.ShapeDtypeStruct((f_loc, dq), F32), jax.ShapeDtypeStruct((1, dq), F32)],
+        in_specs=[vmem] * 4 + [hbm] * 8,
+        out_specs=[vmem, vmem, hbm, hbm, hbm, vmem],
+        scratch_shapes=[
+            pltpu.VMEM((tokens, f_loc), BF16), pltpu.VMEM((tokens, f_loc), BF16), pltpu.VMEM((tokens, f_loc), BF16),
+            pltpu.VMEM((tokens, dq), BF16), pltpu.VMEM((tokens, dq), BF16),
+            pltpu.VMEM((dq, f_loc), BF16), pltpu.VMEM((dq, f_loc), BF16), pltpu.VMEM((f_loc, dq), BF16),
+            pltpu.VMEM((2, NZ, tb, dq), F32), pltpu.VMEM((2, NZ, tb, dq), F32), pltpu.VMEM((2, NZ, tb, dq), F32),
+            pltpu.VMEM((items, SUB, dq), F32), pltpu.VMEM((2 * SUBS, SUB, dq), F32),
+            pltpu.VMEM((dq, f_loc), F32), pltpu.VMEM((dq, f_loc), F32), pltpu.VMEM((f_loc, dq), F32),
+            pltpu.VMEM((tb, 128), F32), pltpu.VMEM((8, tb), F32), pltpu.VMEM((3, 8, tb), F32),
+            pltpu.VMEM((8 * NTY, dq), F32),
+            dma((8,)), dma((items,)), dma((items,)), dma((items,)), dma((items,)), dma((2 * SUBS,)),
+            dma((3, f_loc // 256)), dma((3,)), dma((3,)), dma((NTY,)), dma((NTY,)),
+        ],
+        compiler_params=pltpu.CompilerParams(collective_id=1, has_side_effects=True,
+                                             vmem_limit_bytes=66_500_000),
+        cost_estimate=pl.CostEstimate(flops=12 * tokens * dq * f_loc, bytes_accessed=40_000_000, transcendentals=0),
+    )(x_blk, dy_blk, gain_row, stats, act_all, d_gate_all, d_up_all, hq, dyq, w1, w3, w2)
+
+
 def solution(mesh):
-    tx_size = mesh.shape["tx"]
-
     def local_step(x_blk, dy_blk, gain_blk, w_gate_blk, w_up_blk, w_down_blk):
-        d_model = x_blk.shape[1] * tx_size
         gain_row = gain_blk[None, :]
         act_all, d_gate_all, d_up_all, h_all, dy_all, stats = gather_step(
             x_blk, dy_blk, gain_row, w_gate_blk, w_up_blk, w_down_blk)
-        x_float = x_blk.astype(F32)
-        mean_x, inv_std = stats[:, 0:1], stats[:, 1:2]
-        x_hat = (x_float - mean_x) * inv_std
-        mlp_out = lax.psum_scatter(jnp.dot(act_all, w_down_blk, preferred_element_type=F32),
-                                   "ty", scatter_dimension=0, tiled=True)
-        y_blk = (x_float + mlp_out).astype(BF16)
-        dw_down_blk = contract_rows(act_all, dy_all)
-        dw_gate_blk = contract_rows(h_all, d_gate_all)
-        dw_up_blk = contract_rows(h_all, d_up_all)
-        d_hnorm = lax.psum_scatter(contract_cols(d_gate_all, w_gate_blk) + contract_cols(d_up_all, w_up_blk),
-                                   "ty", scatter_dimension=0, tiled=True)
-        d_xhat = d_hnorm * gain_blk
-        bwd_stats = lax.psum(jnp.stack([jnp.sum(d_xhat, axis=1), jnp.sum(d_xhat * x_hat, axis=1)]), "tx") / d_model
-        dx_ln = inv_std * (d_xhat - bwd_stats[0][:, None] - x_hat * bwd_stats[1][:, None])
-        dx_blk = (dy_blk.astype(F32) + dx_ln).astype(BF16)
-        d_gain_blk = lax.psum(jnp.sum(d_hnorm * x_hat, axis=0), "ty")
-        return (y_blk, dx_blk, dw_gate_blk, dw_up_blk, dw_down_blk, d_gain_blk)
+        y_blk, dx_blk, dw_gate_blk, dw_up_blk, dw_down_blk, d_gain_row = scatter_step(
+            x_blk, dy_blk, gain_row, stats, act_all, d_gate_all, d_up_all, h_all, dy_all,
+            w_gate_blk, w_up_blk, w_down_blk)
+        return (y_blk, dx_blk, dw_gate_blk, dw_up_blk, dw_down_blk, d_gain_row[0])
 
     return jax.shard_map(
         local_step, mesh=mesh,

time: 395 us -> 314 us (0.79)
  waiting for transfers between devices: 158 us -> 0 us
  Pallas kernels: 143 us -> 298 us
  matrix products: 44.3 us -> 0 us
  blocking collectives: 26.9 us -> 0 us
  between operations: 14.1 us -> 0.65 us
  local copies, waits for them, and re-layouts: 4.28 us -> 13.5 us
    reduce_scatter x2 -> x0, waiting for transfers between devices: 158 us -> none  [the longest x1 80.2 us: local_step(): lax.psum_scatter(contract_cols(d_gate_all, w_gate_blk) + contract_cols(d_...]
    pallas_call x0 -> x1, Pallas kernels: none -> 155 us  [scatter_step(): pl.pallas_call(scatter_kernel, out_shape=[jax.ShapeDtypeStruct((tb, dq),...]
    dot_general x6 -> x0, matrix products: 44.3 us -> none  [the longest x3 22.4 us: contract_rows(): lax.dot_general(left_op, right_op, (((0,), (0,)), ((), ())), preferred_el...]
    psum x2 -> x0, blocking collectives: 26.9 us -> none  [the longest x1 20.8 us: local_step(): d_gain_blk = lax.psum(jnp.sum(d_hnorm * x_hat, axis=0), 'ty')]
    unnamed x22 -> x9, local copies, waits for them, and re-layouts: 2.79 us -> 12.3 us
  transfers between devices with their start and end apart: 2 -> 0, of which waited for: 2 -> 0; matrix products, arithmetic and copies ran while one was open for 8% -> 0% of each run, Pallas kernels for 0% -> 0%
where the time goes in v2:
time: 314 us; the launch traced here: 313 us
  Pallas kernels  298 us (95%)
  local copies, waits for them, and re-layouts  13.5 us (4%)
    pallas_call x1, Pallas kernels, scatter_step(): pl.pallas_call(scatter_kernel, out_shape=[jax.ShapeDtypeStruct((tb, dq),...  155 us
    pallas_call x1, Pallas kernels, gather_step(): pl.pallas_call(gather_kernel, out_shape=[jax.ShapeDtypeStruct((tokens, f_...  143 us
    unnamed x9, local copies, waits for them, and re-layouts  12.3 us

profile of v2, /device:TPU:0, one launch (start us, length us, event | category | flops | bytes accessed | tf_op | source)
XLA Modules:
  0.0 313.4 jit_solution(16173928062558395831)
XLA Ops:
  0.6 1.3 broadcast_in_dim.3.gain_ref
  1.9 142.9 %shard_map.109 = (bf16[2048,1280]{1,0:T(8,128)(2,1)}, bf16[2048,1280]{1,0:T(8,128)(2,1)}, bf16[2048,1280]{1,0:T(8,128)(2,1)}, bf16[2048,640]{1,0:T(8,128)(2,1)},...) custom-call(bf16[256,640]{1,0:T(8,128)(2,1)} %x_ref.3, bf16[256,640]{1,0:T(8,128)(2,1)} %dy_ref.3, ...), custom_call_target="tpu_custom_call" | custom-call | flops 20132659200 | bytes 40000000 | tf_op jit(solution)/shard_map/pallas_call | solution.py:309
  144.9 155.0 %shard_map.110 = (bf16[256,640]{1,0:T(8,128)(2,1)}, bf16[256,640]{1,0:T(8,128)(2,1)}, f32[640,1280]{1,0:T(8,128)}, f32[640,1280]{1,0:T(8,128)}, f32[1280,640]{1,0:T(8,128)}, /*index=5*/f32[1,640]{1,0:T(1,128)}) custom-call(bf16[256,640]{1,0:T(8,128)(2,1)} %x_ref.3, bf16[256,640]{1,0:T(8,128)(2,1)} %dy_ref.3, f32[1,640]{1,0:T(1,128)} %broadcast_in_dim.3.gain_ref, ...), custom_call_target="tpu_custom_call" | custom-call | flops 20132659200 | bytes 40000000 | tf_op jit(solution)/shard_map/pallas_call | solution.py:603
  299.9 1.3 reduce
  301.2 1.7 copy.17
  302.9 1.7 copy.18
  304.6 0.0 copy-start.1
  304.6 4.0 %copy.19 = f32[640,1280]{1,0:T(8,128)} copy(f32[640,1280]{1,0:T(8,128)} %get-tuple-element.38) | data formatting | bytes 6553600
  308.6 0.0 copy-done.1
  308.6 0.0 copy-start
  308.6 1.7 copy.20
  310.3 1.4 copy-done
  311.7 1.7 copy.21
Async XLA Ops:
  304.6 4.0 %copy-start.1 = (f32[640,1280]{1,0:T(8,128)S(1)}, f32[640,1280]{1,0:T(8,128)}, u32[]{:S(2)}) copy-start(f32[640,1280]{1,0:T(8,128)} %get-tuple-element.39) | copy-start | bytes 9830404
  308.6 3.1 copy-start

commit v3 on v0

v3 whole, which is shorter than its diff:
```python
import jax
import jax.numpy as jnp
from jax import lax
from jax.experimental import pallas as pl
from jax.experimental.pallas import tpu as pltpu
from jax.sharding import PartitionSpec as P

LN_EPS = 1e-6
MESH = pl.DeviceIdType.MESH
F32 = jnp.float32
BF16 = jnp.bfloat16
NZ = 4
NTY = 8
NTX = 4
SUB = 64
SUBS = 4
ITEMS = 2 * NZ * SUBS
LAG = 2
DW_FIRST = 8
DW_GAP = 2
DW_ROWS = 512


def contract_rows(left_op, right_op):
    return lax.dot_general(left_op, right_op, (((0,), (0,)), ((), ())), preferred_element_type=F32)


def contract_cols(left_op, right_op):
    return lax.dot_general(left_op, right_op, (((1,), (1,)), ((), ())), preferred_element_type=F32)


def matmul(left_op, right_op):
    return jnp.dot(left_op, right_op, preferred_element_type=F32)


def remote(src, dst, send_sem, recv_sem, device):
    return pltpu.make_async_remote_copy(src_ref=src, dst_ref=dst, send_sem=send_sem, recv_sem=recv_sem,
                                        device_id=device, device_id_type=MESH)


def span(index, size):
    return pl.ds(pl.multiple_of(index * size, size), size)


def item_of(i):
    return i // (NZ * SUBS), 3 * (i % (NZ * SUBS) // SUBS) % NZ, i % SUBS


def step_kernel(x_ref, dy_ref, gain_ref, w1_ref, w3_ref, w2_ref,
                y_out, dx_out, dw1_out, dw3_out, dw2_out, dg_out, hg, dyg,
                h_blk, tiles, w1f, w3f, w2f, w2_own, part, v_buf, act, gate_g, up_g, y_recv, z_buf, z_fin, stage,
                st_src, st_buf, pack, sb_src, sb_buf, dg_buf, norm,
                st_s, st_r, x_s, x_r, up_s, dn_s, z_r, y_s, y_r, d_s, d_r, w_s, w_r, w_l, e_s, e_r, t_l, o_l, l_l,
                q_s, q_r, c_s, c_r, f_r, dw_l, sb_s, sb_r, dg_s, dg_r):
    ty, tx = lax.axis_index("ty"), lax.axis_index("tx")
    z, y, core = ty // 2, ty % 2, tx % 2
    yp, up, dn = ty + 1 - 2 * y, ty + 2, ty - 2
    cp, xp, dp = tx + 1 - 2 * core, (tx + 2) % NTX, NTX - 1 - tx
    tx_peers = ((0, cp), (1, xp), (2, dp))
    tb, dq = x_ref.shape
    d_model = dq * NTX
    tokens = tb * NTY
    f_loc = w1_ref.shape[1]
    fh = f_loc // 2
    hi = z // 2
    near = z * (1 - hi) + (NZ - 1 - z) * hi
    far = NZ - 1 - near

    barrier = pltpu.get_barrier_semaphore()
    for _, dev in tx_peers:
        pl.semaphore_signal(barrier, inc=1, device_id=(ty, dev), device_id_type=MESH)
    for r in range(1, NTY):
        pl.semaphore_signal(barrier, inc=1, device_id=((ty + r) % NTY, tx), device_id_type=MESH)

    w_shards = (w1_ref, w3_ref, w2_ref)
    w_full = (w1f, w3f, w2f)

    def w_refs(w, c):
        mine = span(tx, dq)
        if w == 2:
            return w_shards[w].at[span(c, fh), :], w_full[w].at[:, mine]
        return w_shards[w].at[:, span(c, fh)], w_full[w].at[mine, :]

    def w_local(w):
        src, dst = w_refs(w, core)
        return pltpu.make_async_copy(src, dst, w_l.at[w])

    def w_copy(w, r, dev):
        src, dst = w_refs(w, dev % 2)
        return remote(src, dst, w_s.at[w, r], w_r.at[w, r], (ty, dev))

    def w_arrive(w, r, dev):
        theirs = span(dev, dq)
        dst = w_full[w].at[:, theirs] if w == 2 else w_full[w].at[theirs, :]
        return remote(dst, dst, w_s.at[w, r], w_r.at[w, r], (ty, dev))

    def wait_w(w):
        w_local(w).wait()
        for r, dev in tx_peers:
            w_arrive(w, r, dev).wait_recv()

    for w in range(3):
        w_local(w).start()
    w2_own_copy = pltpu.make_async_copy(w2_ref, w2_own, l_l.at[0])
    w2_own_copy.start()
    gathered = (hg, dyg)
    own_blk = (h_blk, dy_ref)

    def block(t, q, row_ty):
        return gathered[t].at[span(row_ty, tb), span(q, dq)]

    def own_local(t):
        return pltpu.make_async_copy(own_blk[t], block(t, tx, ty), o_l.at[t])

    own_local(1).start()

    x_float = x_ref[...].astype(F32)
    lane = lax.broadcasted_iota(jnp.int32, (tb, 128), 1)
    sum_1 = jnp.sum(x_float, axis=1, keepdims=True)
    sum_2 = jnp.sum(x_float * x_float, axis=1, keepdims=True)
    st_src[...] = jnp.where(lane == 0, sum_1, jnp.where(lane == 1, sum_2, 0.0)).T[:8]
    dg_row = span(ty, 8)
    dg_buf[dg_row, :] = jnp.zeros((8, dq), F32)

    pl.semaphore_wait(barrier, NTY + NTX - 2)

    def quarter(s, q):
        return q if s == 0 else (q + 2) % NTX

    def stat_copy(r, dev):
        return remote(st_src, st_buf.at[r], st_s.at[r], st_r.at[r], (ty, dev))

    def x_copy(t):
        return remote(own_blk[t], block(t, tx, ty), x_s.at[t], x_r.at[t], (ty, xp))

    def x_arrive(t):
        ref = block(t, xp, ty)
        return remote(ref, ref, x_s.at[t], x_r.at[t], (ty, xp))

    def z_copy(t, s, layer, sem, dev, own=False):
        ref = block(t, quarter(s, tx), layer * 2 + y)
        return remote(own_blk[t] if own else ref, ref, sem.at[t, s, layer], z_r.at[t, s, layer], (dev, tx))

    def y_copy(t, s, layer, row_ty, own=False):
        ref = block(t, quarter(s, tx), row_ty)
        return remote(own_blk[t] if own else ref, ref, y_s.at[t, s, layer], y_r.at[t, s, layer], (yp, tx))

    def d_copy(t, s, row_ty, q, own=False):
        ref = block(t, quarter(s, q), row_ty)
        return remote(own_blk[t] if own else ref, ref, d_s.at[t, s, row_ty], d_r.at[t, s, row_ty], (ty, cp))

    def spread(t, s, layer, own=False):
        y_copy(t, s, layer, layer * 2 + y, own).start()
        d_copy(t, s, layer * 2 + y, tx, own).start()

    def send_own(t, s):
        @pl.when(z < NZ - 1)
        def _():
            z_copy(t, s, z, up_s, up, s == 0).start()

        @pl.when(z > 0)
        def _():
            z_copy(t, s, z, dn_s, dn, s == 0).start()

        spread(t, s, z, s == 0)

    for r, dev in tx_peers:
        stat_copy(r, dev).start()
    for w in range(3):
        w_copy(w, 0, cp).start()
    x_copy(1).start()
    send_own(1, 0)
    for r, dev in tx_peers:
        stat_copy(r, dev).wait_recv()
    total = st_src[...] + st_buf[0] + st_buf[1] + st_buf[2]
    total = jnp.concatenate([total, jnp.zeros((120, tb), F32)], axis=0).T
    mean_x = total[:, 0:1] / d_model
    inv_std = lax.rsqrt(total[:, 1:2] / d_model - mean_x * mean_x + LN_EPS)
    gain_row = gain_ref[...].reshape(1, dq)
    h_blk[...] = (gain_row * ((x_float - mean_x) * inv_std)).astype(BF16)
    norm[...] = jnp.where(lane == 0, mean_x, jnp.where(lane == 1, inv_std, 0.0))
    own_local(0).start()
    x_copy(0).start()
    send_own(0, 0)
    for w in range(3):
        w_copy(w, 1, xp).start()
        w_copy(w, 2, dp).start()

    for t in (1, 0):
        x_arrive(t).wait_recv()
        send_own(t, 1)
    order = ((1, 0), (0, 0), (1, 1), (0, 1))
    for k in range(1, NZ):
        for t, s in order:
            @pl.when(z >= k)
            def _():
                layer = z - k
                z_copy(t, s, layer, up_s, dn).wait_recv()

                @pl.when(z < NZ - 1)
                def _():
                    z_copy(t, s, layer, up_s, up).start()

                spread(t, s, layer)

            @pl.when(z + k < NZ)
            def _():
                layer = z + k
                z_copy(t, s, layer, dn_s, up).wait_recv()

                @pl.when(z > 0)
                def _():
                    z_copy(t, s, layer, dn_s, dn).start()

                spread(t, s, layer)

    own_local(0).wait()
    own_local(1).wait()

    def layer_of(n):
        m = n % NZ
        base = m + near * (1 - 2 * m) * (1 - m // 2)
        return base + hi * (NZ - 1 - 2 * base)

    def tile_row(n):
        return layer_of(n) * 2 + y + (n // NZ) * (1 - 2 * y)

    def tile_copy(t, n):
        return pltpu.make_async_copy(gathered[t].at[span(tile_row(n), tb), :], tiles.at[n % 2], t_l.at[n % 2])

    def fetch(t, n):
        row_ty = tile_row(n)
        for s in (0, 1):
            d_copy(t, s, row_ty, cp).wait_recv()
        tile_copy(t, n).start()

    def arrive(n):
        @pl.when(n >= NZ)
        def _():
            row_ty, layer = tile_row(n), layer_of(n)
            for t, s in order:
                y_copy(t, s, layer, row_ty).wait_recv()
                d_copy(t, s, row_ty, tx).start()

    swaps = (act, gate_g, up_g)

    def e_copy(i, row_ty):
        rows = span(row_ty, tb)
        return remote(swaps[i].at[0, rows, :], swaps[i].at[1, rows, :], e_s.at[i, row_ty], e_r.at[i, row_ty],
                      (ty, cp))

    wait_w(0)
    wait_w(1)
    fetch(0, 0)

    def up_step(n, _):
        @pl.when(n > 0)
        def _():
            e_copy(0, tile_row(n - 1)).start()

        @pl.when(n < NTY - 1)
        def _():
            arrive(n + 1)
            fetch(0, n + 1)

        row_ty = tile_row(n)
        tile_copy(0, n).wait()
        h_rows = tiles[n % 2]
        gate = matmul(h_rows, w1f[...])
        up_v = matmul(h_rows, w3f[...])
        part[1, row_ty] = gate
        v_buf[row_ty] = up_v
        act[0, span(row_ty, tb), :] = (gate * jax.nn.sigmoid(gate) * up_v).astype(BF16)
        return 0

    lax.fori_loop(0, NTY, up_step, 0)
    e_copy(0, tile_row(NTY - 1)).start()
    hq, dyq = w1f.at[pl.ds(0, tokens), :], w3f.at[pl.ds(0, tokens), :]
    hq_copy = pltpu.make_async_copy(hg.at[:, span(tx, dq)], hq, l_l.at[1])
    dyq_copy = pltpu.make_async_copy(dyg.at[:, span(tx, dq)], dyq, l_l.at[2])
    hq_copy.start()
    dyq_copy.start()
    w2_own_copy.wait()

    def sub_rows(sub):
        return span(sub, SUB)

    def q_copy(i):
        mat, layer, sub = item_of(i)
        return remote(part.at[mat, layer * 2 + 1 - y, sub_rows(sub), :], y_recv.at[mat, layer, sub_rows(sub), :],
                      q_s.at[i], q_r.at[i], (yp, tx))

    def send_block(mat, j):
        for sub in range(SUBS):
            q_copy((mat * NZ + j) * SUBS + sub).start()

    def part_row(jj):
        return (3 * (jj % NZ) % NZ) * 2 + 1 - y + (jj // NZ) * (2 * y - 1)

    def m_step(jj, _):
        row_ty = part_row(jj)
        rows = span(row_ty, tb)
        e_copy(0, row_ty).wait_recv()
        part[0, row_ty] = (matmul(act[0, rows, :], w2_own[span(core, fh), :])
                           + matmul(act[1, rows, :], w2_own[span(1 - core, fh), :]))

        @pl.when(jnp.logical_and(jj > 0, jj <= NZ))
        def _():
            send_block(0, jj - 1)

        return 0

    lax.fori_loop(0, NTY, m_step, 0)

    def c_refs(i):
        mat, layer, sub = item_of(i)
        return part.at[mat, layer * 2 + y, sub_rows(sub), :]

    def c_up(i):
        return remote(c_refs(i), z_buf.at[i], c_s.at[i], c_r.at[i], (up, tx))

    def c_dn(i):
        return remote(c_refs(i), z_buf.at[i], c_s.at[i], c_r.at[i], (dn, tx))

    def c_fin(i):
        mat, _, sub = item_of(i)
        k = mat * SUBS + sub
        return remote(c_refs(i), z_fin.at[k], c_s.at[i], f_r.at[k], (dn, tx))

    def add_to(i, value):
        mat, layer, sub = item_of(i)
        part[mat, layer * 2 + y, sub_rows(sub), :] = part[mat, layer * 2 + y, sub_rows(sub), :] + value

    def add_run(i):
        c_up(i).wait_recv()
        add_to(i, z_buf[i])

    def slot_step(slot):
        @pl.when(slot < ITEMS)
        def _():
            mat, layer, sub = item_of(slot)
            q_copy(slot).wait_recv()
            add_to(slot, y_recv[mat, layer, sub_rows(sub), :])

        i_up = slot - LAG * z
        l_up = item_of(jnp.maximum(i_up, 0))[1]

        @pl.when(jnp.logical_and(jnp.logical_and(i_up >= 0, i_up < ITEMS), l_up > z))
        def _():
            @pl.when(z > 0)
            def _():
                add_run(i_up)

            c_up(i_up).start()

        i_dn = slot - LAG * (NZ - 1 - z)
        l_dn = item_of(jnp.maximum(i_dn, 0))[1]

        @pl.when(jnp.logical_and(jnp.logical_and(i_dn >= 0, i_dn < ITEMS), l_dn < z))
        def _():
            @pl.when(z < NZ - 1)
            def _():
                add_run(i_dn)

            @pl.when(l_dn < z - 1)
            def _():
                c_dn(i_dn).start()

            @pl.when(l_dn == z - 1)
            def _():
                c_fin(i_dn).start()

        i_fin = slot - LAG * far
        l_fin = item_of(jnp.maximum(i_fin, 0))[1]

        @pl.when(jnp.logical_and(jnp.logical_and(i_fin >= 0, i_fin < ITEMS), l_fin == z))
        def _():
            mat, layer, sub = item_of(i_fin)

            @pl.when(z > 0)
            def _():
                add_run(i_fin)

            @pl.when(z < NZ - 1)
            def _():
                c_fin(i_fin).wait_recv()
                add_to(i_fin, z_fin[mat * SUBS + sub])

            rows = sub_rows(sub)

            @pl.when(mat == 0)
            def _():
                y_out[rows, :] = (x_ref[rows, :].astype(F32) + part[0, layer * 2 + y, rows, :]).astype(BF16)

            @pl.when(mat == 1)
            def _():
                d_h = part[1, layer * 2 + y, rows, :]
                x_hat = (x_ref[rows, :].astype(F32) - norm[rows, 0:1]) * norm[rows, 1:2]
                d_xhat = d_h * gain_ref[...].reshape(1, dq)
                sub_lane = lax.broadcasted_iota(jnp.int32, (SUB, 128), 1)
                pack[rows, :] = jnp.where(sub_lane == 0, jnp.sum(d_xhat, axis=1, keepdims=True),
                                          jnp.where(sub_lane == 1, jnp.sum(d_xhat * x_hat, axis=1, keepdims=True), 0.0))
                dg_buf[dg_row, :] = dg_buf[dg_row, :] + jnp.sum((d_h * x_hat).reshape(SUB // 8, 8, dq), axis=0)

    wait_w(2)
    fetch(1, 0)

    def down_step(n, _):
        @pl.when(n > 0)
        def _():
            e_copy(1, tile_row(n - 1)).start()
            e_copy(2, tile_row(n - 1)).start()

        @pl.when(n < NTY - 1)
        def _():
            fetch(1, n + 1)

        row_ty = tile_row(n)
        rows = span(row_ty, tb)
        tile_copy(1, n).wait()
        d_act = contract_cols(tiles[n % 2], w2f[...])
        gate, up_v = part[1, row_ty], v_buf[row_ty]
        sig = jax.nn.sigmoid(gate)
        gate_g[0, rows, :] = (d_act * up_v * sig * (1.0 + gate * (1.0 - sig))).astype(BF16)
        up_g[0, rows, :] = (d_act * (gate * sig)).astype(BF16)

        @pl.when(n % 2 == 1)
        def _():
            slot_step(n // 2)

        return 0

    lax.fori_loop(0, NTY, down_step, 0)
    e_copy(1, tile_row(NTY - 1)).start()
    e_copy(2, tile_row(NTY - 1)).start()
    w1_own, w3_own = w2f.at[:, pl.ds(0, f_loc)], w2f.at[:, pl.ds(f_loc, f_loc)]
    w1_own_copy = pltpu.make_async_copy(w1_ref, w1_own, l_l.at[3])
    w3_own_copy = pltpu.make_async_copy(w3_ref, w3_own, l_l.at[4])
    w1_own_copy.start()
    w3_own_copy.start()
    w1_own_copy.wait()
    w3_own_copy.wait()

    def dh_step(jj, _):
        row_ty = part_row(jj)
        rows = span(row_ty, tb)
        e_copy(1, row_ty).wait_recv()
        e_copy(2, row_ty).wait_recv()
        acc = contract_cols(gate_g[0, rows, :], w1_own[:, span(core, fh)])
        acc += contract_cols(gate_g[1, rows, :], w1_own[:, span(1 - core, fh)])
        acc += contract_cols(up_g[0, rows, :], w3_own[:, span(core, fh)])
        acc += contract_cols(up_g[1, rows, :], w3_own[:, span(1 - core, fh)])
        part[1, row_ty] = acc

        @pl.when(jnp.logical_and(jj > 0, jj <= NZ))
        def _():
            send_block(1, jj - 1)

        @pl.when(jj % 2 == 1)
        def _():
            slot_step(NTY // 2 + jj // 2)

        return 0

    lax.fori_loop(0, NTY, dh_step, 0)
    hq_copy.wait()
    dyq_copy.wait()

    def dw_copy(c, w):
        half = c % 2
        cols = span(core + half * (1 - 2 * core), fh)
        dst = (dw2_out.at[cols, :], dw1_out.at[:, cols], dw3_out.at[:, cols])[w]
        return pltpu.make_async_copy(stage, dst, dw_l.at[0])

    def weight_grads(slot):
        c = (slot - DW_FIRST) // DW_GAP
        half = c % 2

        def over_tokens(left, right):
            def piece(k, _):
                rows = span(k, DW_ROWS)
                stage[...] = stage[...] + contract_rows(left[rows, :], right[rows, :])
                return 0

            stage[...] = jnp.zeros(stage.shape, F32)
            lax.fori_loop(0, tokens // DW_ROWS, piece, 0)

        @pl.when(jnp.logical_and((slot - DW_FIRST) % DW_GAP == 0, slot < DW_FIRST + 6 * DW_GAP))
        def _():
            @pl.when(c >= 1)
            def _():
                dw_copy(c, 0).wait()

            for w in range(3):
                @pl.when(c // 2 == w)
                def _():
                    over_tokens(act.at[half] if w == 0 else hq, (dyq, gate_g.at[half], up_g.at[half])[w])
                    dw_copy(c, w).start()

    def last_slots(slot, _):
        weight_grads(slot)
        slot_step(slot)
        return 0

    lax.fori_loop(NTY, ITEMS + LAG * (NZ - 2), last_slots, 0)

    def dg_copy(r, row):
        ref = dg_buf.at[span(row, 8), :]
        return remote(ref, ref, dg_s.at[r], dg_r.at[row], ((ty + r) % NTY, tx))

    def sb_copy(r, dev):
        return remote(sb_src, sb_buf.at[r], sb_s.at[r], sb_r.at[r], (ty, dev))

    sb_src[...] = pack[...].T[:8]
    for r in range(1, NTY):
        dg_copy(r, ty).start()
    for r, dev in tx_peers:
        sb_copy(r, dev).start()
    inv_std = norm[:, 1:2]
    x_hat = (x_ref[...].astype(F32) - norm[:, 0:1]) * inv_std
    d_xhat = part[1, ty] * gain_ref[...].reshape(1, dq)
    for r, dev in tx_peers:
        sb_copy(r, dev).wait_recv()
    total = sb_src[...] + sb_buf[0] + sb_buf[1] + sb_buf[2]
    total = jnp.concatenate([total, jnp.zeros((120, tb), F32)], axis=0).T / d_model
    dx_ln = inv_std * (d_xhat - total[:, 0:1] - x_hat * total[:, 1:2])
    dx_out[...] = (dy_ref[...].astype(F32) + dx_ln).astype(BF16)
    for r in range(1, NTY):
        dg_copy(r, (ty + NTY - r) % NTY).wait_recv()
    dg_out[...] = jnp.sum(dg_buf[...], axis=0)

    dw_copy(0, 0).wait()
    for r in range(1, NTY):
        dg_copy(r, ty).wait_send()
    for r, dev in tx_peers:
        sb_copy(r, dev).wait_send()
        stat_copy(r, dev).wait_send()
        for w in range(3):
            w_copy(w, r, dev).wait_send()
    for t in (0, 1):
        x_copy(t).wait_send()

    def drain(layer, _):
        for t, s in order:
            @pl.when(jnp.logical_and(z < NZ - 1, layer <= z))
            def _():
                z_copy(t, s, layer, up_s, up).wait_send()

            @pl.when(jnp.logical_and(z > 0, layer >= z))
            def _():
                z_copy(t, s, layer, dn_s, dn).wait_send()

            y_copy(t, s, layer, layer * 2 + y).wait_send()
            d_copy(t, s, layer * 2, tx).wait_send()
            d_copy(t, s, layer * 2 + 1, tx).wait_send()
        return 0

    lax.fori_loop(0, NZ, drain, 0)

    def drain_swap(row_ty, _):
        for i in range(3):
            e_copy(i, row_ty).wait_send()
        return 0

    lax.fori_loop(0, NTY, drain_swap, 0)

    def drain_items(i, _):
        q_copy(i).wait_send()
        layer = item_of(i)[1]

        @pl.when(layer > z)
        def _():
            c_up(i).wait_send()

        @pl.when(layer < z)
        def _():
            c_dn(i).wait_send()

        return 0

    lax.fori_loop(0, ITEMS, drain_items, 0)


def solution(mesh):
    def local_step(x_blk, dy_blk, gain_blk, w1, w3, w2):
        tb, dq = x_blk.shape
        tokens, d_model, f_loc = tb * NTY, dq * NTX, w1.shape[1]
        fh = f_loc // 2
        dma = pltpu.SemaphoreType.DMA
        vmem = pl.BlockSpec(memory_space=pltpu.VMEM)
        hbm = pl.BlockSpec(memory_space=pl.ANY)
        outs = pl.pallas_call(
            step_kernel,
            out_shape=[
                jax.ShapeDtypeStruct((tb, dq), BF16), jax.ShapeDtypeStruct((tb, dq), BF16),
                jax.ShapeDtypeStruct((dq, f_loc), F32), jax.ShapeDtypeStruct((dq, f_loc), F32),
                jax.ShapeDtypeStruct((f_loc, dq), F32), jax.ShapeDtypeStruct((dq,), F32),
                jax.ShapeDtypeStruct((tokens, d_model), BF16), jax.ShapeDtypeStruct((tokens, d_model), BF16)],
            in_specs=[vmem, vmem, vmem, hbm, hbm, hbm],
            out_specs=[vmem, vmem, hbm, hbm, hbm, vmem, hbm, hbm],
            scratch_shapes=[
                pltpu.VMEM((tb, dq), BF16), pltpu.VMEM((2, tb, d_model), BF16),
                pltpu.VMEM((d_model, fh), BF16), pltpu.VMEM((d_model, fh), BF16), pltpu.VMEM((fh, d_model), BF16),
                pltpu.VMEM((f_loc, dq), BF16),
                pltpu.VMEM((2, NTY, tb, dq), F32), pltpu.VMEM((NTY, tb, fh), F32),
                pltpu.VMEM((2, tokens, fh), BF16), pltpu.VMEM((2, tokens, fh), BF16), pltpu.VMEM((2, tokens, fh), BF16),
                pltpu.VMEM((2, NZ, tb, dq), F32), pltpu.VMEM((ITEMS, SUB, dq), F32), pltpu.VMEM((2 * SUBS, SUB, dq), F32),
                pltpu.VMEM((fh, dq), F32),
                pltpu.VMEM((8, tb), F32), pltpu.VMEM((3, 8, tb), F32),
                pltpu.VMEM((tb, 128), F32), pltpu.VMEM((8, tb), F32), pltpu.VMEM((3, 8, tb), F32),
                pltpu.VMEM((8 * NTY, dq), F32), pltpu.VMEM((tb, 128), F32),
                dma((3,)), dma((3,)), dma((2,)), dma((2,)),
                dma((2, 2, NZ)), dma((2, 2, NZ)), dma((2, 2, NZ)), dma((2, 2, NZ)), dma((2, 2, NZ)),
                dma((2, 2, NTY)), dma((2, 2, NTY)),
                dma((3, 3)), dma((3, 3)), dma((3,)),
                dma((3, NTY)), dma((3, NTY)), dma((2,)), dma((2,)), dma((5,)),
                dma((ITEMS,)), dma((ITEMS,)), dma((ITEMS,)), dma((ITEMS,)), dma((2 * SUBS,)),
                dma((1,)), dma((3,)), dma((3,)), dma((NTY,)), dma((NTY,)),
            ],
            compiler_params=pltpu.CompilerParams(collective_id=0, has_side_effects=True,
                                                 vmem_limit_bytes=67_000_000),
            cost_estimate=pl.CostEstimate(flops=24 * tokens * d_model * fh, bytes_accessed=80_000_000,
                                          transcendentals=2 * tokens * fh),
        )(x_blk, dy_blk, gain_blk, w1, w3, w2)
        return tuple(outs[:6])

    return jax.shard_map(
        local_step, mesh=mesh,
        in_specs=(P("ty", "tx"), P("ty", "tx"), P("tx"), P("tx", "ty"), P("tx", "ty"), P("ty", "tx")),
        out_specs=(P("ty", "tx"), P("ty", "tx"), P("tx", "ty"), P("tx", "ty"), P("ty", "tx"), P("tx")),
        check_vma=False)
```

time: 748 us -> 281 us (0.38)
  waiting for transfers between devices: 593 us -> 0 us
  Pallas kernels: 0 us -> 267 us
  matrix products: 82.3 us -> 0 us
  blocking collectives: 35.3 us -> 0 us
  other arithmetic: 13.9 us -> 0 us
  between operations: 14.4 us -> 0.65 us
  local copies, waits for them, and re-layouts: 0.06 us -> 12.9 us
    reduce_scatter x5 -> x0, waiting for transfers between devices: 398 us -> none  [the longest x1 85.9 us: local_step(): lax.psum_scatter(jnp.dot(h_all, w_gate_blk, preferred_element_type=jnp.fl...]
    pallas_call x0 -> x1, Pallas kernels: none -> 267 us  [local_step(): pl.pallas_call(step_kernel, out_shape=[jax.ShapeDtypeStruct((tb, dq), BF1...]
    all_gather x5 -> x0, waiting for transfers between devices: 193 us -> none  [the longest x1 54 us: local_step(): h_all = lax.all_gather(h_blk, 'ty', axis=0, tiled=True)]
    dot_general x9 -> x0, matrix products: 82.3 us -> none  [the longest x3 30.7 us: contract_cols(): lax.dot_general(left_op, right_op, (((1,), (1,)), ((), ())), preferred_el...]
    psum x3 -> x0, blocking collectives: 35.3 us -> none  [the longest x1 20.8 us: local_step(): d_gain_blk = lax.psum(jnp.sum(d_hnorm * x_hat, axis=0), 'ty')]
    unnamed x18 -> x12, local copies, waits for them, and re-layouts: 0.05 us -> 12.9 us
    convert_element_type x3 -> x0, other arithmetic: 11.1 us -> none  [the longest x1 6.79 us: local_step(): d_up = (d_act * gate_swish).astype(jnp.bfloat16)]
  transfers between devices with their start and end apart: 10 -> 0, of which waited for: 10 -> 0; matrix products, arithmetic and copies ran while one was open for 11% -> 0% of each run, Pallas kernels for 0% -> 0%
where the time goes in v3:
time: 281 us; the launch traced here: 280 us
  Pallas kernels  267 us (95%)
  local copies, waits for them, and re-layouts  12.9 us (5%)
    pallas_call x1, Pallas kernels, local_step(): pl.pallas_call(step_kernel, out_shape=[jax.ShapeDtypeStruct((tb, dq), BF1...  267 us
    unnamed x12, local copies, waits for them, and re-layouts  12.9 us

profile of v3, /device:TPU:0, one launch (start us, length us, event | category | flops | bytes accessed | tf_op | source)
XLA Modules:
  0.0 280.3 jit_solution(5984104775922623514)
XLA Ops:
  0.6 266.7 %shard_map.109 = (bf16[256,640]{1,0:T(8,128)(2,1)}, bf16[256,640]{1,0:T(8,128)(2,1)}, f32[640,1280]{1,0:T(8,128)}, f32[640,1280]{1,0:T(8,128)}, f32[1280,640]{1,...) custom-call(bf16[256,640]{1,0:T(8,128)(2,1)} %x_ref.1, bf16[256,640]{1,0:T(8,128)(2,1)} %dy_ref.1, ...), custom_call_target="tpu_custom_call" | custom-call | flops 80530636800 | bytes 80000000 | tf_op jit(solution)/shard_map/pallas_call | solution.py:592
  267.4 1.7 copy.18
  269.1 1.7 copy.19
  270.8 0.0 copy-start.1
  270.8 4.0 %copy.20 = f32[640,1280]{1,0:T(8,128)} copy(f32[640,1280]{1,0:T(8,128)} %get-tuple-element.26) | data formatting | bytes 6553600
  274.8 0.0 copy-done.1
  274.8 0.0 copy-start
  274.8 1.7 copy.21
  276.5 1.4 copy-done
  277.9 0.0 copy-start.2
  278.0 1.7 copy.22
  279.7 0.0 copy-done.2
  279.7 0.6 copy.23
Async XLA Ops:
  270.8 4.0 %copy-start.1 = (f32[640,1280]{1,0:T(8,128)S(1)}, f32[640,1280]{1,0:T(8,128)}, u32[]{:S(2)}) copy-start(f32[640,1280]{1,0:T(8,128)} %get-tuple-element.27) | copy-start | bytes 9830404
  274.8 3.1 %copy-start = (f32[1280,640]{1,0:T(8,128)S(1)}, f32[1280,640]{1,0:T(8,128)}, u32[]{:S(2)}) copy-start(f32[1280,640]{1,0:T(8,128)} %get-tuple-element.28) | copy-start | bytes 9830404
  277.9 1.7 copy-start.2

commit v4 on v3

--- a/solution.py
+++ b/solution.py
@@ -12,12 +12,12 @@
 NZ = 4
 NTY = 8
 NTX = 4
-SUB = 64
-SUBS = 4
+SUB = 32
+SUBS = 8
 ITEMS = 2 * NZ * SUBS
 LAG = 2
-DW_FIRST = 8
-DW_GAP = 2
+DW_FIRST = 16
+DW_GAP = 4
 DW_ROWS = 512
 
 
@@ -50,7 +50,7 @@
                 y_out, dx_out, dw1_out, dw3_out, dw2_out, dg_out, hg, dyg,
                 h_blk, tiles, w1f, w3f, w2f, w2_own, part, v_buf, act, gate_g, up_g, y_recv, z_buf, z_fin, stage,
                 st_src, st_buf, pack, sb_src, sb_buf, dg_buf, norm,
-                st_s, st_r, x_s, x_r, up_s, dn_s, z_r, y_s, y_r, d_s, d_r, w_s, w_r, w_l, e_s, e_r, t_l, o_l, l_l,
+                st_s, st_r, x_s, x_r, up_s, dn_s, z_r, uo_s, do_s, zo_r, y_s, y_r, d_s, d_r, w_s, w_r, w_l, e_s, e_r, t_l, o_l, l_l,
                 q_s, q_r, c_s, c_r, f_r, dw_l, sb_s, sb_r, dg_s, dg_r):
     ty, tx = lax.axis_index("ty"), lax.axis_index("tx")
     z, y, core = ty // 2, ty % 2, tx % 2
@@ -186,34 +186,76 @@
         w_copy(w, 1, xp).start()
         w_copy(w, 2, dp).start()
 
+    def zo_copy(layer, sem, dev):
+        ref = block(1, quarter(1, tx), layer * 2 + 1 - y)
+        return remote(ref, ref, sem.at[layer], zo_r.at[layer], (dev, tx))
+
+    order = ((0, 0), (0, 1), (1, 0), (1, 1))
+
+    def pass_up(layer, copy, sem, after):
+        copy(layer, sem, dn).wait_recv()
+
+        @pl.when(z < NZ - 1)
+        def _():
+            copy(layer, sem, up).start()
+
+        after(layer)
+
+    def pass_down(layer, copy, sem, after):
+        copy(layer, sem, up).wait_recv()
+
+        @pl.when(z > 0)
+        def _():
+            copy(layer, sem, dn).start()
+
+        after(layer)
+
+    def relay(k, t, s):
+        def copy(layer, sem, dev):
+            return z_copy(t, s, layer, sem, dev)
+
+        def after(layer):
+            if (t, s) != (1, 1):
+                y_copy(t, s, layer, layer * 2 + y).start()
+            d_copy(t, s, layer * 2 + y, tx).start()
+
+        def after_other(layer):
+            d_copy(1, 1, layer * 2 + 1 - y, tx).start()
+
+        @pl.when(z >= k)
+        def _():
+            pass_up(z - k, copy, up_s, after)
+            if (t, s) == (1, 1):
+                pass_up(z - k, zo_copy, uo_s, after_other)
+
+        @pl.when(z + k < NZ)
+        def _():
+            pass_down(z + k, copy, dn_s, after)
+            if (t, s) == (1, 1):
+                pass_down(z + k, zo_copy, do_s, after_other)
+
     for t in (1, 0):
         x_arrive(t).wait_recv()
         send_own(t, 1)
-    order = ((1, 0), (0, 0), (1, 1), (0, 1))
-    for k in range(1, NZ):
-        for t, s in order:
-            @pl.when(z >= k)
-            def _():
-                layer = z - k
-                z_copy(t, s, layer, up_s, dn).wait_recv()
-
-                @pl.when(z < NZ - 1)
-                def _():
-                    z_copy(t, s, layer, up_s, up).start()
-
-                spread(t, s, layer)
-
-            @pl.when(z + k < NZ)
-            def _():
-                layer = z + k
-                z_copy(t, s, layer, dn_s, up).wait_recv()
-
-                @pl.when(z > 0)
-                def _():
-                    z_copy(t, s, layer, dn_s, dn).start()
-
-                spread(t, s, layer)
-
+    for s in (0, 1):
+        relay(1, 0, s)
+    y_copy(1, 1, z, ty + 1 - 2 * y).wait_recv()
+
+    @pl.when(z < NZ - 1)
+    def _():
+        zo_copy(z, uo_s, up).start()
+
+    @pl.when(z > 0)
+    def _():
+        zo_copy(z, do_s, dn).start()
+
+    d_copy(1, 1, yp, tx).start()
+    for s in (0, 1):
+        relay(2, 0, s)
+    for s in (0, 1):
+        relay(1, 1, s)
+    for s in (0, 1):
+        relay(3, 0, s)
     own_local(0).wait()
     own_local(1).wait()
 
@@ -225,22 +267,14 @@
     def tile_row(n):
         return layer_of(n) * 2 + y + (n // NZ) * (1 - 2 * y)
 
-    def tile_copy(t, n):
-        return pltpu.make_async_copy(gathered[t].at[span(tile_row(n), tb), :], tiles.at[n % 2], t_l.at[n % 2])
-
-    def fetch(t, n):
-        row_ty = tile_row(n)
-        for s in (0, 1):
-            d_copy(t, s, row_ty, cp).wait_recv()
-        tile_copy(t, n).start()
-
-    def arrive(n):
-        @pl.when(n >= NZ)
-        def _():
-            row_ty, layer = tile_row(n), layer_of(n)
-            for t, s in order:
-                y_copy(t, s, layer, row_ty).wait_recv()
-                d_copy(t, s, row_ty, tx).start()
+    chip = tx // 2
+
+    def tile_copy(t, n, half=None):
+        rows = span(tile_row(n), tb)
+        if half is None:
+            return pltpu.make_async_copy(gathered[t].at[rows, :], tiles.at[n % 2], t_l.at[n % 2])
+        return pltpu.make_async_copy(gathered[t].at[rows, span(half, 2 * dq)], tiles.at[n % 2, :, pl.ds(0, 2 * dq)],
+                                     t_l.at[n % 2])
 
     swaps = (act, gate_g, up_g)
 
@@ -249,37 +283,72 @@
         return remote(swaps[i].at[0, rows, :], swaps[i].at[1, rows, :], e_s.at[i, row_ty], e_r.at[i, row_ty],
                       (ty, cp))
 
-    wait_w(0)
-    wait_w(1)
-    fetch(0, 0)
-
-    def up_step(n, _):
+    def fetch_near(n):
+        row_ty = tile_row(n)
+
+        @pl.when(n >= NZ)
+        def _():
+            for s in (0, 1):
+                y_copy(0, s, layer_of(n), row_ty).wait_recv()
+                d_copy(0, s, row_ty, tx).start()
+
+        d_copy(0, 0, row_ty, cp).wait_recv()
+        tile_copy(0, n, chip).start()
+
+    def fetch_far(n):
+        d_copy(0, 1, tile_row(n), cp).wait_recv()
+        tile_copy(0, n, 1 - chip).start()
+
+    def near_step(n, _):
+        @pl.when(n < NTY - 1)
+        def _():
+            fetch_near(n + 1)
+
+        row_ty = tile_row(n)
+        tile_copy(0, n, chip).wait()
+        h_rows = tiles[n % 2, :, pl.ds(0, 2 * dq)]
+        part[1, row_ty] = matmul(h_rows, w1f[span(chip, 2 * dq), :])
+        v_buf[row_ty] = matmul(h_rows, w3f[span(chip, 2 * dq), :])
+        return 0
+
+    for w in (0, 1):
+        w_local(w).wait()
+        w_arrive(w, 0, cp).wait_recv()
+    fetch_near(0)
+    lax.fori_loop(0, NTY, near_step, 0)
+    for s in (0, 1):
+        relay(2, 1, s)
+    for w in (0, 1):
+        w_arrive(w, 1, xp).wait_recv()
+        w_arrive(w, 2, dp).wait_recv()
+    fetch_far(0)
+
+    def far_step(n, _):
         @pl.when(n > 0)
         def _():
             e_copy(0, tile_row(n - 1)).start()
 
         @pl.when(n < NTY - 1)
         def _():
-            arrive(n + 1)
-            fetch(0, n + 1)
+            fetch_far(n + 1)
 
         row_ty = tile_row(n)
-        tile_copy(0, n).wait()
-        h_rows = tiles[n % 2]
-        gate = matmul(h_rows, w1f[...])
-        up_v = matmul(h_rows, w3f[...])
+        tile_copy(0, n, 1 - chip).wait()
+        h_rows = tiles[n % 2, :, pl.ds(0, 2 * dq)]
+        gate = part[1, row_ty] + matmul(h_rows, w1f[span(1 - chip, 2 * dq), :])
+        up_v = v_buf[row_ty] + matmul(h_rows, w3f[span(1 - chip, 2 * dq), :])
         part[1, row_ty] = gate
         v_buf[row_ty] = up_v
         act[0, span(row_ty, tb), :] = (gate * jax.nn.sigmoid(gate) * up_v).astype(BF16)
         return 0
 
-    lax.fori_loop(0, NTY, up_step, 0)
+    lax.fori_loop(0, NTY, far_step, 0)
+    relay(3, 1, 0)
     e_copy(0, tile_row(NTY - 1)).start()
     hq, dyq = w1f.at[pl.ds(0, tokens), :], w3f.at[pl.ds(0, tokens), :]
     hq_copy = pltpu.make_async_copy(hg.at[:, span(tx, dq)], hq, l_l.at[1])
     dyq_copy = pltpu.make_async_copy(dyg.at[:, span(tx, dq)], dyq, l_l.at[2])
     hq_copy.start()
-    dyq_copy.start()
     w2_own_copy.wait()
 
     def sub_rows(sub):
@@ -311,6 +380,16 @@
         return 0
 
     lax.fori_loop(0, NTY, m_step, 0)
+    relay(3, 1, 1)
+
+    def dy_arrive(layer, _):
+        row_ty = layer * 2 + 1 - y
+        y_copy(1, 0, layer, row_ty).wait_recv()
+        d_copy(1, 0, row_ty, tx).start()
+        return 0
+
+    lax.fori_loop(0, NZ, dy_arrive, 0)
+    dyq_copy.start()
 
     def c_refs(i):
         mat, layer, sub = item_of(i)
@@ -402,8 +481,13 @@
                                           jnp.where(sub_lane == 1, jnp.sum(d_xhat * x_hat, axis=1, keepdims=True), 0.0))
                 dg_buf[dg_row, :] = dg_buf[dg_row, :] + jnp.sum((d_h * x_hat).reshape(SUB // 8, 8, dq), axis=0)
 
+    def fetch_dy(n):
+        for s in (0, 1):
+            d_copy(1, s, tile_row(n), cp).wait_recv()
+        tile_copy(1, n).start()
+
     wait_w(2)
-    fetch(1, 0)
+    fetch_dy(0)
 
     def down_step(n, _):
         @pl.when(n > 0)
@@ -413,7 +497,7 @@
 
         @pl.when(n < NTY - 1)
         def _():
-            fetch(1, n + 1)
+            fetch_dy(n + 1)
 
         row_ty = tile_row(n)
         rows = span(row_ty, tb)
@@ -424,10 +508,7 @@
         gate_g[0, rows, :] = (d_act * up_v * sig * (1.0 + gate * (1.0 - sig))).astype(BF16)
         up_g[0, rows, :] = (d_act * (gate * sig)).astype(BF16)
 
-        @pl.when(n % 2 == 1)
-        def _():
-            slot_step(n // 2)
-
+        slot_step(n)
         return 0
 
     lax.fori_loop(0, NTY, down_step, 0)
@@ -456,10 +537,7 @@
         def _():
             send_block(1, jj - 1)
 
-        @pl.when(jj % 2 == 1)
-        def _():
-            slot_step(NTY // 2 + jj // 2)
-
+        slot_step(NTY + jj)
         return 0
 
     lax.fori_loop(0, NTY, dh_step, 0)
@@ -502,7 +580,7 @@
         slot_step(slot)
         return 0
 
-    lax.fori_loop(NTY, ITEMS + LAG * (NZ - 2), last_slots, 0)
+    lax.fori_loop(2 * NTY, ITEMS + LAG * (NZ - 2), last_slots, 0)
 
     def dg_copy(r, row):
         ref = dg_buf.at[span(row, 8), :]
@@ -550,11 +628,22 @@
             def _():
                 z_copy(t, s, layer, dn_s, dn).wait_send()
 
-            y_copy(t, s, layer, layer * 2 + y).wait_send()
+            if (t, s) != (1, 1):
+                y_copy(t, s, layer, layer * 2 + y).wait_send()
             d_copy(t, s, layer * 2, tx).wait_send()
             d_copy(t, s, layer * 2 + 1, tx).wait_send()
-        return 0
-
+
+        @pl.when(jnp.logical_and(z < NZ - 1, layer <= z))
+        def _():
+            zo_copy(layer, uo_s, up).wait_send()
+
+        @pl.when(jnp.logical_and(z > 0, layer >= z))
+        def _():
+            zo_copy(layer, do_s, dn).wait_send()
+
+        return 0
+
+    y_copy(1, 1, z, ty).wait_send()
     lax.fori_loop(0, NZ, drain, 0)
 
     def drain_swap(row_ty, _):
@@ -579,6 +668,50 @@
         return 0
 
     lax.fori_loop(0, ITEMS, drain_items, 0)
+
+
+def pieces_of(arrays):
+    out = []
+    for n, array in enumerate(arrays):
+        cuts = 4 if array.shape[0] * array.shape[1] > 400_000 else 1
+        rows = array.shape[0] // cuts
+        out += [(n, pl.ds(c * rows, rows)) for c in range(cuts)]
+    return out
+
+
+def hand_out_kernel(*refs):
+    k = (len(refs) - 4) // 3
+    gain_in, ins, gain_out, outs = refs[0], refs[1:1 + k], refs[1 + k], refs[2 + k:2 + 2 * k]
+    bufs, (in_sem, out_sem) = refs[2 + 2 * k:2 + 3 * k], refs[2 + 3 * k:]
+    pieces = pieces_of(ins)
+    loads = [pltpu.make_async_copy(ins[n].at[rows, :], bufs[n].at[rows, :], in_sem.at[c])
+             for c, (n, rows) in enumerate(pieces)]
+    stores = [pltpu.make_async_copy(bufs[n].at[rows, :], outs[n].at[rows, :], out_sem.at[c])
+              for c, (n, rows) in enumerate(pieces)]
+    for load in loads:
+        load.start()
+    gain_out[...] = gain_in[...]
+    for load, store in zip(loads, stores):
+        load.wait()
+        store.start()
+    for store in stores:
+        store.wait()
+
+
+def hand_out(gain, arrays):
+    k = len(arrays)
+    vmem = pl.BlockSpec(memory_space=pltpu.VMEM)
+    hbm = pl.BlockSpec(memory_space=pl.ANY)
+    n_pieces = len(pieces_of(arrays))
+    return pl.pallas_call(
+        hand_out_kernel,
+        out_shape=[jax.ShapeDtypeStruct(a.shape, a.dtype) for a in (gain, *arrays)],
+        in_specs=[vmem] + [hbm] * k,
+        out_specs=[vmem] + [hbm] * k,
+        scratch_shapes=[pltpu.VMEM(a.shape, a.dtype) for a in arrays]
+        + [pltpu.SemaphoreType.DMA((n_pieces,)), pltpu.SemaphoreType.DMA((n_pieces,))],
+        compiler_params=pltpu.CompilerParams(vmem_limit_bytes=60_000_000),
+    )(gain, *arrays)
 
 
 def solution(mesh):
@@ -610,7 +743,8 @@
                 pltpu.VMEM((tb, 128), F32), pltpu.VMEM((8, tb), F32), pltpu.VMEM((3, 8, tb), F32),
                 pltpu.VMEM((8 * NTY, dq), F32), pltpu.VMEM((tb, 128), F32),
                 dma((3,)), dma((3,)), dma((2,)), dma((2,)),
-                dma((2, 2, NZ)), dma((2, 2, NZ)), dma((2, 2, NZ)), dma((2, 2, NZ)), dma((2, 2, NZ)),
+                dma((2, 2, NZ)), dma((2, 2, NZ)), dma((2, 2, NZ)), dma((NZ,)), dma((NZ,)), dma((NZ,)),
+                dma((2, 2, NZ)), dma((2, 2, NZ)),
                 dma((2, 2, NTY)), dma((2, 2, NTY)),
                 dma((3, 3)), dma((3, 3)), dma((3,)),
                 dma((3, NTY)), dma((3, NTY)), dma((2,)), dma((2,)), dma((5,)),
@@ -622,7 +756,8 @@
             cost_estimate=pl.CostEstimate(flops=24 * tokens * d_model * fh, bytes_accessed=80_000_000,
                                           transcendentals=2 * tokens * fh),
         )(x_blk, dy_blk, gain_blk, w1, w3, w2)
-        return tuple(outs[:6])
+        d_gain_blk, *rest = hand_out(outs[5], outs[:5])
+        return (*rest, d_gain_blk)
 
     return jax.shard_map(
         local_step, mesh=mesh,

time: 281 us -> 276 us (0.982)
  local copies, waits for them, and re-layouts: 12.9 us -> 0 us
  Pallas kernels: 267 us -> 275 us
    unnamed x12 -> x0, local copies, waits for them, and re-layouts: 12.9 us -> none
    pallas_call x0 -> x1, Pallas kernels: none -> 9.21 us  [hand_out(): pl.pallas_call(hand_out_kernel, out_shape=[jax.ShapeDtypeStruct(a.shape,...]
where the time goes in v4:
time: 276 us
  Pallas kernels  275 us (100%)
    pallas_call x1, Pallas kernels, local_step(): pl.pallas_call(step_kernel, out_shape=[jax.ShapeDtypeStruct((tb, dq), BF1...  266 us
    pallas_call x1, Pallas kernels, hand_out(): pl.pallas_call(hand_out_kernel, out_shape=[jax.ShapeDtypeStruct(a.shape,...  9.21 us

profile of v4, /device:TPU:0, one launch (start us, length us, event | category | flops | bytes accessed | tf_op | source)
XLA Modules:
  0.0 275.6 jit_solution(5921277441206804859)
XLA Ops:
  0.6 265.7 %shard_map.109 = (bf16[256,640]{1,0:T(8,128)(2,1)}, bf16[256,640]{1,0:T(8,128)(2,1)}, f32[640,1280]{1,0:T(8,128)}, f32[640,1280]{1,0:T(8,128)}, f32[1280,640]{1,...) custom-call(bf16[256,640]{1,0:T(8,128)(2,1)} %x_ref.1, bf16[256,640]{1,0:T(8,128)(2,1)} %dy_ref.1, ...), custom_call_target="tpu_custom_call" | custom-call | flops 80530636800 | bytes 80000000 | tf_op jit(solution)/shard_map/pallas_call | solution.py:725
  266.4 9.2 %shard_map.110 = (f32[640]{0:T(1024)}, bf16[256,640]{1,0:T(8,128)(2,1)}, bf16[256,640]{1,0:T(8,128)(2,1)}, f32[640,1280]{1,0:T(8,128)}, f32[640,1280]{1,0:T(8,128)}, /*index=5*/f32[1280,640]{1,0:T(8,128)}) custom-call(f32[640]{0:T(1024)} %get-tuple-element.18.refs_0_, bf16[256,640]{1,0:T(8,128)(2,1)} %get-tuple-element.19.refs_1_, ...), custom_call_target="tpu_custom_call" | custom-call | tf_op jit(solution)/shard_map/pallas_call | solution.py:706

commit v5 on v4

--- a/solution.py
+++ b/solution.py
@@ -15,9 +15,9 @@
 SUB = 32
 SUBS = 8
 ITEMS = 2 * NZ * SUBS
-LAG = 2
-DW_FIRST = 16
-DW_GAP = 4
+LAG = 3
+DW_FIRST = 28
+DW_GAP = 3
 DW_ROWS = 512
 
 
@@ -43,7 +43,12 @@
 
 
 def item_of(i):
-    return i // (NZ * SUBS), 3 * (i % (NZ * SUBS) // SUBS) % NZ, i % SUBS
+    e = i % (NZ * SUBS)
+    return i // (NZ * SUBS), pair_layer(e // (2 * SUBS), e % 2), e % (2 * SUBS) // 2
+
+
+def pair_layer(pair, side):
+    return pair + side * (NZ - 1 - 2 * pair)
 
 
 def step_kernel(x_ref, dy_ref, gain_ref, w1_ref, w3_ref, w2_ref,
@@ -359,12 +364,12 @@
         return remote(part.at[mat, layer * 2 + 1 - y, sub_rows(sub), :], y_recv.at[mat, layer, sub_rows(sub), :],
                       q_s.at[i], q_r.at[i], (yp, tx))
 
-    def send_block(mat, j):
-        for sub in range(SUBS):
-            q_copy((mat * NZ + j) * SUBS + sub).start()
+    def send_pair(mat, pair):
+        for e in range(2 * SUBS):
+            q_copy((mat * 2 + pair) * 2 * SUBS + e).start()
 
     def part_row(jj):
-        return (3 * (jj % NZ) % NZ) * 2 + 1 - y + (jj // NZ) * (2 * y - 1)
+        return pair_layer(jj % NZ // 2, jj % 2) * 2 + 1 - y + (jj // NZ) * (2 * y - 1)
 
     def m_step(jj, _):
         row_ty = part_row(jj)
@@ -373,9 +378,9 @@
         part[0, row_ty] = (matmul(act[0, rows, :], w2_own[span(core, fh), :])
                            + matmul(act[1, rows, :], w2_own[span(1 - core, fh), :]))
 
-        @pl.when(jnp.logical_and(jj > 0, jj <= NZ))
-        def _():
-            send_block(0, jj - 1)
+        @pl.when(jnp.logical_and(jj % 2 == 0, jnp.logical_and(jj > 0, jj <= NZ)))
+        def _():
+            send_pair(0, jj // 2 - 1)
 
         return 0
 
@@ -486,6 +491,11 @@
             d_copy(1, s, tile_row(n), cp).wait_recv()
         tile_copy(1, n).start()
 
+    def early_slots(slot, _):
+        slot_step(slot)
+        return 0
+
+    lax.fori_loop(0, NTY, early_slots, 0)
     wait_w(2)
     fetch_dy(0)
 
@@ -508,7 +518,7 @@
         gate_g[0, rows, :] = (d_act * up_v * sig * (1.0 + gate * (1.0 - sig))).astype(BF16)
         up_g[0, rows, :] = (d_act * (gate * sig)).astype(BF16)
 
-        slot_step(n)
+        slot_step(NTY + n)
         return 0
 
     lax.fori_loop(0, NTY, down_step, 0)
@@ -533,11 +543,11 @@
         acc += contract_cols(up_g[1, rows, :], w3_own[:, span(1 - core, fh)])
         part[1, row_ty] = acc
 
-        @pl.when(jnp.logical_and(jj > 0, jj <= NZ))
-        def _():
-            send_block(1, jj - 1)
-
-        slot_step(NTY + jj)
+        @pl.when(jnp.logical_and(jj % 2 == 0, jnp.logical_and(jj > 0, jj <= NZ)))
+        def _():
+            send_pair(1, jj // 2 - 1)
+
+        slot_step(2 * NTY + jj)
         return 0
 
     lax.fori_loop(0, NTY, dh_step, 0)
@@ -580,7 +590,7 @@
         slot_step(slot)
         return 0
 
-    lax.fori_loop(2 * NTY, ITEMS + LAG * (NZ - 2), last_slots, 0)
+    lax.fori_loop(3 * NTY, ITEMS + LAG * (NZ - 2), last_slots, 0)
 
     def dg_copy(r, row):
         ref = dg_buf.at[span(row, 8), :]

time: 276 us -> 257 us (0.931)
  Pallas kernels: 275 us -> 256 us
    pallas_call x1, Pallas kernels: 266 us -> 247 us  [local_step(): pl.pallas_call(step_kernel, out_shape=[jax.ShapeDtypeStruct((tb, dq), BF1...]
where the time goes in v5:
time: 257 us
  Pallas kernels  256 us (100%)
    pallas_call x1, Pallas kernels, local_step(): pl.pallas_call(step_kernel, out_shape=[jax.ShapeDtypeStruct((tb, dq), BF1...  247 us
    pallas_call x1, Pallas kernels, hand_out(): pl.pallas_call(hand_out_kernel, out_shape=[jax.ShapeDtypeStruct(a.shape,...  9.21 us

profile of v5, /device:TPU:0, one launch (start us, length us, event | category | flops | bytes accessed | tf_op | source)
XLA Modules:
  0.0 256.5 jit_solution(13209795667466397600)
XLA Ops:
  0.6 246.7 %shard_map.109 = (bf16[256,640]{1,0:T(8,128)(2,1)}, bf16[256,640]{1,0:T(8,128)(2,1)}, f32[640,1280]{1,0:T(8,128)}, f32[640,1280]{1,0:T(8,128)}, f32[1280,640]{1,...) custom-call(bf16[256,640]{1,0:T(8,128)(2,1)} %x_ref.1, bf16[256,640]{1,0:T(8,128)(2,1)} %dy_ref.1, ...), custom_call_target="tpu_custom_call" | custom-call | flops 80530636800 | bytes 80000000 | tf_op jit(solution)/shard_map/pallas_call | solution.py:735
  247.3 9.2 %shard_map.110 = (f32[640]{0:T(1024)}, bf16[256,640]{1,0:T(8,128)(2,1)}, bf16[256,640]{1,0:T(8,128)(2,1)}, f32[640,1280]{1,0:T(8,128)}, f32[640,1280]{1,0:T(8,128)}, /*index=5*/f32[1280,640]{1,0:T(8,128)}) custom-call(f32[640]{0:T(1024)} %get-tuple-element.18.refs_0_, bf16[256,640]{1,0:T(8,128)(2,1)} %get-tuple-element.19.refs_1_, ...), custom_call_target="tpu_custom_call" | custom-call | tf_op jit(solution)/shard_map/pallas_call | solution.py:716

commit v6 on v5

--- a/solution.py
+++ b/solution.py
@@ -19,6 +19,8 @@
 DW_FIRST = 28
 DW_GAP = 3
 DW_ROWS = 512
+DRAIN_LAG = 24
+DRAIN_SLOT = 46
 
 
 def contract_rows(left_op, right_op):
@@ -300,10 +302,6 @@
         d_copy(0, 0, row_ty, cp).wait_recv()
         tile_copy(0, n, chip).start()
 
-    def fetch_far(n):
-        d_copy(0, 1, tile_row(n), cp).wait_recv()
-        tile_copy(0, n, 1 - chip).start()
-
     def near_step(n, _):
         @pl.when(n < NTY - 1)
         def _():
@@ -326,50 +324,47 @@
     for w in (0, 1):
         w_arrive(w, 1, xp).wait_recv()
         w_arrive(w, 2, dp).wait_recv()
-    fetch_far(0)
-
-    def far_step(n, _):
-        @pl.when(n > 0)
-        def _():
-            e_copy(0, tile_row(n - 1)).start()
-
-        @pl.when(n < NTY - 1)
-        def _():
-            fetch_far(n + 1)
-
-        row_ty = tile_row(n)
-        tile_copy(0, n, 1 - chip).wait()
-        h_rows = tiles[n % 2, :, pl.ds(0, 2 * dq)]
+    def sub_rows(sub):
+        return span(sub, SUB)
+
+    def q_copy(i):
+        mat, layer, sub = item_of(i)
+        return remote(part.at[mat, layer * 2 + 1 - y, sub_rows(sub), :], y_recv.at[mat, layer, sub_rows(sub), :],
+                      q_s.at[i], q_r.at[i], (yp, tx))
+
+    def send_pair(mat, pair):
+        for e in range(2 * SUBS):
+            q_copy((mat * 2 + pair) * 2 * SUBS + e).start()
+
+    def part_row(jj):
+        return pair_layer(jj % NZ // 2, jj % 2) * 2 + 1 - y + (jj // NZ) * (2 * y - 1)
+
+    def far_copy(jj):
+        src = hg.at[span(part_row(jj), tb), span(1 - chip, 2 * dq)]
+        return pltpu.make_async_copy(src, tiles.at[jj % 2, :, pl.ds(0, 2 * dq)], t_l.at[jj % 2])
+
+    def fetch_far(jj):
+        d_copy(0, 1, part_row(jj), cp).wait_recv()
+        far_copy(jj).start()
+
+    def far_step(jj, _):
+        @pl.when(jj % 2 == 1)
+        def _():
+            e_copy(0, part_row(jj - 1)).start()
+
+        @pl.when(jj < NTY - 1)
+        def _():
+            fetch_far(jj + 1)
+
+        row_ty = part_row(jj)
+        far_copy(jj).wait()
+        h_rows = tiles[jj % 2, :, pl.ds(0, 2 * dq)]
         gate = part[1, row_ty] + matmul(h_rows, w1f[span(1 - chip, 2 * dq), :])
         up_v = v_buf[row_ty] + matmul(h_rows, w3f[span(1 - chip, 2 * dq), :])
         part[1, row_ty] = gate
         v_buf[row_ty] = up_v
         act[0, span(row_ty, tb), :] = (gate * jax.nn.sigmoid(gate) * up_v).astype(BF16)
         return 0
-
-    lax.fori_loop(0, NTY, far_step, 0)
-    relay(3, 1, 0)
-    e_copy(0, tile_row(NTY - 1)).start()
-    hq, dyq = w1f.at[pl.ds(0, tokens), :], w3f.at[pl.ds(0, tokens), :]
-    hq_copy = pltpu.make_async_copy(hg.at[:, span(tx, dq)], hq, l_l.at[1])
-    dyq_copy = pltpu.make_async_copy(dyg.at[:, span(tx, dq)], dyq, l_l.at[2])
-    hq_copy.start()
-    w2_own_copy.wait()
-
-    def sub_rows(sub):
-        return span(sub, SUB)
-
-    def q_copy(i):
-        mat, layer, sub = item_of(i)
-        return remote(part.at[mat, layer * 2 + 1 - y, sub_rows(sub), :], y_recv.at[mat, layer, sub_rows(sub), :],
-                      q_s.at[i], q_r.at[i], (yp, tx))
-
-    def send_pair(mat, pair):
-        for e in range(2 * SUBS):
-            q_copy((mat * 2 + pair) * 2 * SUBS + e).start()
-
-    def part_row(jj):
-        return pair_layer(jj % NZ // 2, jj % 2) * 2 + 1 - y + (jj // NZ) * (2 * y - 1)
 
     def m_step(jj, _):
         row_ty = part_row(jj)
@@ -377,14 +372,31 @@
         e_copy(0, row_ty).wait_recv()
         part[0, row_ty] = (matmul(act[0, rows, :], w2_own[span(core, fh), :])
                            + matmul(act[1, rows, :], w2_own[span(1 - core, fh), :]))
-
-        @pl.when(jnp.logical_and(jj % 2 == 0, jnp.logical_and(jj > 0, jj <= NZ)))
-        def _():
-            send_pair(0, jj // 2 - 1)
-
-        return 0
-
-    lax.fori_loop(0, NTY, m_step, 0)
+        return 0
+
+    def two_tiles(g, _):
+        lax.fori_loop(2 * g, 2 * g + 2, far_step, 0)
+        e_copy(0, part_row(2 * g + 1)).start()
+        lax.fori_loop(2 * g, 2 * g + 2, m_step, 0)
+
+        @pl.when(g == 0)
+        def _():
+            relay(3, 1, 0)
+
+        @pl.when(g < 2)
+        def _():
+            send_pair(0, g)
+
+        return 0
+
+    w2_own_copy.wait()
+    fetch_far(0)
+    lax.fori_loop(0, NTY // 2, two_tiles, 0)
+    hq, dyq = w1f.at[pl.ds(0, tokens), :], w3f.at[pl.ds(0, tokens), :]
+    hq_copy = pltpu.make_async_copy(hg.at[:, span(tx, dq)], hq, l_l.at[1])
+    dyq_copy = pltpu.make_async_copy(dyg.at[:, span(tx, dq)], dyq, l_l.at[2])
+    hq_copy.start()
+
     relay(3, 1, 1)
 
     def dy_arrive(layer, _):
@@ -585,9 +597,71 @@
                     over_tokens(act.at[half] if w == 0 else hq, (dyq, gate_g.at[half], up_g.at[half])[w])
                     dw_copy(c, w).start()
 
+    def drain_gathers():
+        for r, dev in tx_peers:
+            stat_copy(r, dev).wait_send()
+            for w in range(3):
+                w_copy(w, r, dev).wait_send()
+        for t in (0, 1):
+            x_copy(t).wait_send()
+        y_copy(1, 1, z, ty).wait_send()
+
+        def drain_layer(layer, _):
+            for t, s in order:
+                @pl.when(jnp.logical_and(z < NZ - 1, layer <= z))
+                def _():
+                    z_copy(t, s, layer, up_s, up).wait_send()
+
+                @pl.when(jnp.logical_and(z > 0, layer >= z))
+                def _():
+                    z_copy(t, s, layer, dn_s, dn).wait_send()
+
+                if (t, s) != (1, 1):
+                    y_copy(t, s, layer, layer * 2 + y).wait_send()
+                d_copy(t, s, layer * 2, tx).wait_send()
+                d_copy(t, s, layer * 2 + 1, tx).wait_send()
+
+            @pl.when(jnp.logical_and(z < NZ - 1, layer <= z))
+            def _():
+                zo_copy(layer, uo_s, up).wait_send()
+
+            @pl.when(jnp.logical_and(z > 0, layer >= z))
+            def _():
+                zo_copy(layer, do_s, dn).wait_send()
+
+            return 0
+
+        def drain_swap(row_ty, _):
+            for i in range(3):
+                e_copy(i, row_ty).wait_send()
+            return 0
+
+        lax.fori_loop(0, NZ, drain_layer, 0)
+        lax.fori_loop(0, NTY, drain_swap, 0)
+
+    def drain_item(i, _):
+        q_copy(i).wait_send()
+        layer = item_of(i)[1]
+
+        @pl.when(layer > z)
+        def _():
+            c_up(i).wait_send()
+
+        @pl.when(layer < z)
+        def _():
+            c_dn(i).wait_send()
+
+        return 0
+
     def last_slots(slot, _):
         weight_grads(slot)
         slot_step(slot)
+        drain_item(slot - DRAIN_LAG, 0)
+
+        @pl.when(slot == DRAIN_SLOT)
+        def _():
+            drain_gathers()
+
         return 0
 
     lax.fori_loop(3 * NTY, ITEMS + LAG * (NZ - 2), last_slots, 0)
@@ -622,62 +696,7 @@
         dg_copy(r, ty).wait_send()
     for r, dev in tx_peers:
         sb_copy(r, dev).wait_send()
-        stat_copy(r, dev).wait_send()
-        for w in range(3):
-            w_copy(w, r, dev).wait_send()
-    for t in (0, 1):
-        x_copy(t).wait_send()
-
-    def drain(layer, _):
-        for t, s in order:
-            @pl.when(jnp.logical_and(z < NZ - 1, layer <= z))
-            def _():
-                z_copy(t, s, layer, up_s, up).wait_send()
-
-            @pl.when(jnp.logical_and(z > 0, layer >= z))
-            def _():
-                z_copy(t, s, layer, dn_s, dn).wait_send()
-
-            if (t, s) != (1, 1):
-                y_copy(t, s, layer, layer * 2 + y).wait_send()
-            d_copy(t, s, layer * 2, tx).wait_send()
-            d_copy(t, s, layer * 2 + 1, tx).wait_send()
-
-        @pl.when(jnp.logical_and(z < NZ - 1, layer <= z))
-        def _():
-            zo_copy(layer, uo_s, up).wait_send()
-
-        @pl.when(jnp.logical_and(z > 0, layer >= z))
-        def _():
-            zo_copy(layer, do_s, dn).wait_send()
-
-        return 0
-
-    y_copy(1, 1, z, ty).wait_send()
-    lax.fori_loop(0, NZ, drain, 0)
-
-    def drain_swap(row_ty, _):
-        for i in range(3):
-            e_copy(i, row_ty).wait_send()
-        return 0
-
-    lax.fori_loop(0, NTY, drain_swap, 0)
-
-    def drain_items(i, _):
-        q_copy(i).wait_send()
-        layer = item_of(i)[1]
-
-        @pl.when(layer > z)
-        def _():
-            c_up(i).wait_send()
-
-        @pl.when(layer < z)
-        def _():
-            c_dn(i).wait_send()
-
-        return 0
-
-    lax.fori_loop(0, ITEMS, drain_items, 0)
+    lax.fori_loop(ITEMS + LAG * (NZ - 2) - DRAIN_LAG, ITEMS, drain_item, 0)
 
 
 def pieces_of(arrays):

time: 257 us -> 250 us (0.973)
  Pallas kernels: 256 us -> 250 us
    pallas_call x1, Pallas kernels: 247 us -> 240 us  [local_step(): pl.pallas_call(step_kernel, out_shape=[jax.ShapeDtypeStruct((tb, dq), BF1...]
where the time goes in v6:
time: 250 us
  Pallas kernels  250 us (100%)
    pallas_call x1, Pallas kernels, local_step(): pl.pallas_call(step_kernel, out_shape=[jax.ShapeDtypeStruct((tb, dq), BF1...  240 us
    pallas_call x1, Pallas kernels, hand_out(): pl.pallas_call(hand_out_kernel, out_shape=[jax.ShapeDtypeStruct(a.shape,...  9.21 us

profile of v6, /device:TPU:0, one launch (start us, length us, event | category | flops | bytes accessed | tf_op | source)
XLA Modules:
  0.0 250.2 jit_solution(14267028554819385542)
XLA Ops:
  0.6 240.4 %shard_map.109 = (bf16[256,640]{1,0:T(8,128)(2,1)}, bf16[256,640]{1,0:T(8,128)(2,1)}, f32[640,1280]{1,0:T(8,128)}, f32[640,1280]{1,0:T(8,128)}, f32[1280,640]{1,...) custom-call(bf16[256,640]{1,0:T(8,128)(2,1)} %x_ref.1, bf16[256,640]{1,0:T(8,128)(2,1)} %dy_ref.1, ...), custom_call_target="tpu_custom_call" | custom-call | flops 80530636800 | bytes 80000000 | tf_op jit(solution)/shard_map/pallas_call | solution.py:754
  241.0 9.2 %shard_map.110 = (f32[640]{0:T(1024)}, bf16[256,640]{1,0:T(8,128)(2,1)}, bf16[256,640]{1,0:T(8,128)(2,1)}, f32[640,1280]{1,0:T(8,128)}, f32[640,1280]{1,0:T(8,128)}, /*index=5*/f32[1280,640]{1,0:T(8,128)}) custom-call(f32[640]{0:T(1024)} %get-tuple-element.18.refs_0_, bf16[256,640]{1,0:T(8,128)(2,1)} %get-tuple-element.19.refs_1_, ...), custom_call_target="tpu_custom_call" | custom-call | tf_op jit(solution)/shard_map/pallas_call | solution.py:735

commit v7 on v6

--- a/solution.py
+++ b/solution.py
@@ -217,7 +217,7 @@
 
         after(layer)
 
-    def relay(k, t, s):
+    def relay(k, t, s, main=True, other=False):
         def copy(layer, sem, dev):
             return z_copy(t, s, layer, sem, dev)
 
@@ -231,14 +231,16 @@
 
         @pl.when(z >= k)
         def _():
-            pass_up(z - k, copy, up_s, after)
-            if (t, s) == (1, 1):
+            if main:
+                pass_up(z - k, copy, up_s, after)
+            if other:
                 pass_up(z - k, zo_copy, uo_s, after_other)
 
         @pl.when(z + k < NZ)
         def _():
-            pass_down(z + k, copy, dn_s, after)
-            if (t, s) == (1, 1):
+            if main:
+                pass_down(z + k, copy, dn_s, after)
+            if other:
                 pass_down(z + k, zo_copy, do_s, after_other)
 
     for t in (1, 0):
@@ -246,7 +248,13 @@
         send_own(t, 1)
     for s in (0, 1):
         relay(1, 0, s)
-    y_copy(1, 1, z, ty + 1 - 2 * y).wait_recv()
+    for s in (0, 1):
+        relay(2, 0, s)
+    relay(1, 1, 0)
+    for s in (0, 1):
+        relay(3, 0, s)
+    relay(2, 1, 0)
+    y_copy(1, 1, z, yp).wait_recv()
 
     @pl.when(z < NZ - 1)
     def _():
@@ -257,12 +265,7 @@
         zo_copy(z, do_s, dn).start()
 
     d_copy(1, 1, yp, tx).start()
-    for s in (0, 1):
-        relay(2, 0, s)
-    for s in (0, 1):
-        relay(1, 1, s)
-    for s in (0, 1):
-        relay(3, 0, s)
+    relay(1, 1, 1)
     own_local(0).wait()
     own_local(1).wait()
 
@@ -319,8 +322,8 @@
         w_arrive(w, 0, cp).wait_recv()
     fetch_near(0)
     lax.fori_loop(0, NTY, near_step, 0)
-    for s in (0, 1):
-        relay(2, 1, s)
+    relay(1, 1, 1, main=False, other=True)
+    relay(3, 1, 0)
     for w in (0, 1):
         w_arrive(w, 1, xp).wait_recv()
         w_arrive(w, 2, dp).wait_recv()
@@ -379,13 +382,13 @@
         e_copy(0, part_row(2 * g + 1)).start()
         lax.fori_loop(2 * g, 2 * g + 2, m_step, 0)
 
+        @pl.when(g < 2)
+        def _():
+            send_pair(0, g)
+
         @pl.when(g == 0)
         def _():
-            relay(3, 1, 0)
-
-        @pl.when(g < 2)
-        def _():
-            send_pair(0, g)
+            relay(2, 1, 1, other=True)
 
         return 0
 
@@ -397,7 +400,7 @@
     dyq_copy = pltpu.make_async_copy(dyg.at[:, span(tx, dq)], dyq, l_l.at[2])
     hq_copy.start()
 
-    relay(3, 1, 1)
+    relay(3, 1, 1, other=True)
 
     def dy_arrive(layer, _):
         row_ty = layer * 2 + 1 - y

time: 250 us -> 248 us (level)
  Pallas kernels: 250 us -> 247 us
    pallas_call x1, Pallas kernels: 240 us -> 238 us  [local_step(): pl.pallas_call(step_kernel, out_shape=[jax.ShapeDtypeStruct((tb, dq), BF1...]
where the time goes in v7:
time: 248 us
  Pallas kernels  247 us (100%)
    pallas_call x1, Pallas kernels, local_step(): pl.pallas_call(step_kernel, out_shape=[jax.ShapeDtypeStruct((tb, dq), BF1...  238 us
    pallas_call x1, Pallas kernels, hand_out(): pl.pallas_call(hand_out_kernel, out_shape=[jax.ShapeDtypeStruct(a.shape,...  9.21 us

profile of v7, /device:TPU:0, one launch (start us, length us, event | category | flops | bytes accessed | tf_op | source)
XLA Modules:
  0.0 247.6 jit_solution(11240494313829595130)
XLA Ops:
  0.6 237.6 %shard_map.109 = (bf16[256,640]{1,0:T(8,128)(2,1)}, bf16[256,640]{1,0:T(8,128)(2,1)}, f32[640,1280]{1,0:T(8,128)}, f32[640,1280]{1,0:T(8,128)}, f32[1280,640]{1,...) custom-call(bf16[256,640]{1,0:T(8,128)(2,1)} %x_ref.1, bf16[256,640]{1,0:T(8,128)(2,1)} %dy_ref.1, ...), custom_call_target="tpu_custom_call" | custom-call | flops 80530636800 | bytes 80000000 | tf_op jit(solution)/shard_map/pallas_call | solution.py:757
  238.3 9.2 %shard_map.110 = (f32[640]{0:T(1024)}, bf16[256,640]{1,0:T(8,128)(2,1)}, bf16[256,640]{1,0:T(8,128)(2,1)}, f32[640,1280]{1,0:T(8,128)}, f32[640,1280]{1,0:T(8,128)}, /*index=5*/f32[1280,640]{1,0:T(8,128)}) custom-call(f32[640]{0:T(1024)} %get-tuple-element.18.refs_0_, bf16[256,640]{1,0:T(8,128)(2,1)} %get-tuple-element.19.refs_1_, ...), custom_call_target="tpu_custom_call" | custom-call | tf_op jit(solution)/shard_map/pallas_call | solution.py:738

commit v8 on v7

--- a/solution.py
+++ b/solution.py
@@ -12,15 +12,15 @@
 NZ = 4
 NTY = 8
 NTX = 4
-SUB = 32
-SUBS = 8
+SUB = 16
+SUBS = 16
 ITEMS = 2 * NZ * SUBS
-LAG = 3
-DW_FIRST = 28
-DW_GAP = 3
+LAG = 5
+DW_FIRST = 56
+DW_GAP = 6
 DW_ROWS = 512
-DRAIN_LAG = 24
-DRAIN_SLOT = 46
+DRAIN_LAG = 48
+DRAIN_SLOT = 92
 
 
 def contract_rows(left_op, right_op):
@@ -510,7 +510,7 @@
         slot_step(slot)
         return 0
 
-    lax.fori_loop(0, NTY, early_slots, 0)
+    lax.fori_loop(0, 2 * NTY, early_slots, 0)
     wait_w(2)
     fetch_dy(0)
 
@@ -533,7 +533,7 @@
         gate_g[0, rows, :] = (d_act * up_v * sig * (1.0 + gate * (1.0 - sig))).astype(BF16)
         up_g[0, rows, :] = (d_act * (gate * sig)).astype(BF16)
 
-        slot_step(NTY + n)
+        lax.fori_loop(2 * (NTY + n), 2 * (NTY + n) + 2, early_slots, 0)
         return 0
 
     lax.fori_loop(0, NTY, down_step, 0)
@@ -562,7 +562,7 @@
         def _():
             send_pair(1, jj // 2 - 1)
 
-        slot_step(2 * NTY + jj)
+        lax.fori_loop(2 * (2 * NTY + jj), 2 * (2 * NTY + jj) + 2, early_slots, 0)
         return 0
 
     lax.fori_loop(0, NTY, dh_step, 0)
@@ -667,7 +667,7 @@
 
         return 0
 
-    lax.fori_loop(3 * NTY, ITEMS + LAG * (NZ - 2), last_slots, 0)
+    lax.fori_loop(6 * NTY, ITEMS + LAG * (NZ - 2), last_slots, 0)
 
     def dg_copy(r, row):
         ref = dg_buf.at[span(row, 8), :]

time: 248 us -> 257 us (1.036)
  Pallas kernels: 247 us -> 256 us
    pallas_call x1, Pallas kernels: 238 us -> 247 us  [local_step(): pl.pallas_call(step_kernel, out_shape=[jax.ShapeDtypeStruct((tb, dq), BF1...]
where the time goes in v8:
time: 257 us
  Pallas kernels  256 us (100%)
    pallas_call x1, Pallas kernels, local_step(): pl.pallas_call(step_kernel, out_shape=[jax.ShapeDtypeStruct((tb, dq), BF1...  247 us
    pallas_call x1, Pallas kernels, hand_out(): pl.pallas_call(hand_out_kernel, out_shape=[jax.ShapeDtypeStruct(a.shape,...  9.21 us

profile of v8, /device:TPU:0, one launch (start us, length us, event | category | flops | bytes accessed | tf_op | source)
XLA Modules:
  0.0 256.5 jit_solution(14568711723994108944)
XLA Ops:
  0.6 246.5 %shard_map.109 = (bf16[256,640]{1,0:T(8,128)(2,1)}, bf16[256,640]{1,0:T(8,128)(2,1)}, f32[640,1280]{1,0:T(8,128)}, f32[640,1280]{1,0:T(8,128)}, f32[1280,640]{1,...) custom-call(bf16[256,640]{1,0:T(8,128)(2,1)} %x_ref.1, bf16[256,640]{1,0:T(8,128)(2,1)} %dy_ref.1, ...), custom_call_target="tpu_custom_call" | custom-call | flops 80530636800 | bytes 80000000 | tf_op jit(solution)/shard_map/pallas_call | solution.py:757
  247.2 9.2 %shard_map.110 = (f32[640]{0:T(1024)}, bf16[256,640]{1,0:T(8,128)(2,1)}, bf16[256,640]{1,0:T(8,128)(2,1)}, f32[640,1280]{1,0:T(8,128)}, f32[640,1280]{1,0:T(8,128)}, /*index=5*/f32[1280,640]{1,0:T(8,128)}) custom-call(f32[640]{0:T(1024)} %get-tuple-element.18.refs_0_, bf16[256,640]{1,0:T(8,128)(2,1)} %get-tuple-element.19.refs_1_, ...), custom_call_target="tpu_custom_call" | custom-call | tf_op jit(solution)/shard_map/pallas_call | solution.py:738
